TPU v7x, 16 devices: a 4x2x1 block of a 4x4x8 slice. The times are simulated.
16 devices in a mesh: dp: 2 (over y, z), sp: 8 (over x, core).
Axes of the slice: x: 4, y: 2, z: 1, core: 2. Of those that a mesh axis runs over, the one named last changes fastest.
The devices are a block of a 4x4x8 slice.
Arguments:
- dec_hidden: bfloat16 [2048, 512], P(('dp', 'sp')), parts along dimension 0
- enc_memory: bfloat16 [16384, 512], P(('dp', 'sp')), parts along dimension 0
- mem_len: int32 [2], P('dp'), parts along dimension 0
- norm_self: bfloat16 [2, 512], replicated
- norm_cross: bfloat16 [2, 512], replicated
- norm_mlp: bfloat16 [2, 512], replicated
- self_q: bfloat16 [2, 512, 512], replicated
- self_k: bfloat16 [2, 512, 512], replicated
- self_v: bfloat16 [2, 512, 512], replicated
- self_o: bfloat16 [2, 8, 64, 512], replicated
- cross_q: bfloat16 [2, 512, 512], replicated
- cross_k: bfloat16 [2, 512, 512], replicated
- cross_v: bfloat16 [2, 512, 512], replicated
- cross_o: bfloat16 [2, 8, 64, 512], replicated
- mlp_gate: bfloat16 [2, 512, 2048], replicated
- mlp_up: bfloat16 [2, 512, 2048], replicated
- mlp_down: bfloat16 [2, 2048, 512], replicated
Outputs:
- output: bfloat16 [2048, 512], P(('dp', 'sp')), parts along dimension 0
There are 2 independent parts. A program takes and returns all parts, laid end to end along the dimension named above; an argument that names none is the same for every part.
All inputs are finite; a program needn't handle non-finite values.
Results may differ from a plain program's by a relative error of at most 0.0152673.
Values are sent between devices in bfloat16 or wider.
A program may use at most 768 MiB of HBM per device.

v0:
```python
import jax
import jax.numpy as jnp
from jax import lax
from jax.sharding import PartitionSpec as P

EPS = 1e-6
NEG_BIG = -1e30


def rms_norm(hidden, gain_vec):
    hidden32 = hidden.astype(jnp.float32)
    inv_rms = lax.rsqrt(jnp.mean(hidden32 * hidden32, axis=-1, keepdims=True) + EPS)
    return (hidden32 * inv_rms * gain_vec.astype(jnp.float32)).astype(jnp.bfloat16)


def project(acts, weight_mat):
    return jnp.dot(acts, weight_mat, preferred_element_type=jnp.float32).astype(jnp.bfloat16)


def add_residual(hidden, update):
    return (hidden.astype(jnp.float32) + update).astype(jnp.bfloat16)


def solution(mesh):
    group = mesh.shape['sp']
    row_spec = P(('dp', 'sp'), None)

    def local_step(hidden, memory, mem_len, norm_self, norm_cross, norm_mlp, self_q, self_k, self_v, self_o, cross_q, cross_k, cross_v, cross_o, mlp_gate, mlp_up, mlp_down):
        rows, width = hidden.shape
        mem_rows = memory.shape[0]
        n_heads, head_dim = self_o.shape[1], self_o.shape[2]
        kv_heads = cross_k.shape[2] // head_dim
        n_groups = n_heads // kv_heads
        all_rows = rows * group
        soft_scale = head_dim ** -0.5
        shard_index = lax.axis_index('sp')
        query_pos = shard_index * rows + jnp.arange(rows)
        causal = query_pos[:, None] >= jnp.arange(all_rows)[None, :]
        mem_valid = (shard_index * mem_rows + jnp.arange(mem_rows)) < mem_len[0]
        for layer in range(norm_self.shape[0]):
            normed = rms_norm(hidden, norm_self[layer])
            queries = project(normed, self_q[layer]).reshape(rows, n_heads, head_dim)
            keys_all = lax.all_gather(project(normed, self_k[layer]), 'sp', axis=0, tiled=True).reshape(all_rows, n_heads, head_dim)
            values_all = lax.all_gather(project(normed, self_v[layer]), 'sp', axis=0, tiled=True).reshape(all_rows, n_heads, head_dim)
            scores = jnp.einsum('thd,shd->hts', queries, keys_all, preferred_element_type=jnp.float32) * soft_scale
            scores = jnp.where(causal, scores, NEG_BIG)
            weights = jnp.exp(scores - jnp.max(scores, axis=-1, keepdims=True))
            numerator = jnp.einsum('hts,shd->htd', weights.astype(jnp.bfloat16), values_all, preferred_element_type=jnp.float32)
            attended = (numerator / jnp.sum(weights, axis=-1, keepdims=True)).astype(jnp.bfloat16)
            hidden = add_residual(hidden, jnp.einsum('htd,hdo->to', attended, self_o[layer], preferred_element_type=jnp.float32))

            normed = rms_norm(hidden, norm_cross[layer])
            cross_queries = lax.all_gather(project(normed, cross_q[layer]), 'sp', axis=0, tiled=True).reshape(all_rows, kv_heads, n_groups, head_dim)
            mem_keys = project(memory, cross_k[layer]).reshape(mem_rows, kv_heads, head_dim)
            mem_values = project(memory, cross_v[layer]).reshape(mem_rows, kv_heads, head_dim)
            scores = jnp.einsum('tkgd,skd->kgts', cross_queries, mem_keys, preferred_element_type=jnp.float32) * soft_scale
            scores = jnp.where(mem_valid, scores, NEG_BIG)
            part_max = jnp.max(scores, axis=-1, keepdims=True)
            weights = jnp.exp(scores - part_max)
            part_sum = jnp.sum(weights, axis=-1, keepdims=True)
            part_num = jnp.einsum('kgts,skd->kgtd', weights.astype(jnp.bfloat16), mem_values, preferred_element_type=jnp.float32)
            rescale = jnp.exp(part_max - lax.pmax(part_max, 'sp'))
            packed = jnp.concatenate([part_num * rescale, part_sum * rescale], axis=-1)
            combined = lax.psum_scatter(packed, 'sp', scatter_dimension=2, tiled=True)
            attended = (combined[..., :head_dim] / combined[..., head_dim:]).astype(jnp.bfloat16)
            out_heads = cross_o[layer].reshape(kv_heads, n_groups, head_dim, width)
            hidden = add_residual(hidden, jnp.einsum('kgtd,kgdo->to', attended, out_heads, preferred_element_type=jnp.float32))

            normed = rms_norm(hidden, norm_mlp[layer])
            gate_pre = jnp.dot(normed, mlp_gate[layer], preferred_element_type=jnp.float32)
            up_proj = jnp.dot(normed, mlp_up[layer], preferred_element_type=jnp.float32)
            hidden_act = (jax.nn.silu(gate_pre) * up_proj).astype(jnp.bfloat16)
            hidden = add_residual(hidden, jnp.dot(hidden_act, mlp_down[layer], preferred_element_type=jnp.float32))
        return hidden

    return jax.shard_map(local_step, mesh=mesh, in_specs=(row_spec, row_spec, P('dp')) + (P(),) * 14, out_specs=row_spec, check_vma=False)
```

profile of v0, /device:TPU:127, one launch (start us, length us, event | category | flops | bytes accessed | tf_op | source)
XLA Modules:
  0.0 364.6 jit_solution(6145493157798793447)
XLA Ops:
  7.3 1.0 fusion.139
  8.4 2.0 convolution_convert_fusion.10
  10.6 2.0 convolution_convert_fusion.9
  12.7 1.4 convolution_convert_fusion.11
  15.2 14.3 %all-gather.7.cloned.1.call-done = bf16[1024,512]{1,0:T(8,128)(2,1)} async-done(((bf16[128,512]{1,0:T(8,128)(2,1)}), bf16[1024,512]{1,0:T(8,128)(2,1)}) %all-gather.7.cloned.1.call-update) | async-done | bytes 1048592 | tf_op jit(solution)/shard_map/all_gather | solution.py:43
  29.5 1.5 copy.27
  32.0 1.9 copy-done.3
  33.9 1.7 fusion.16
  35.5 14.4 %all-gather.9.cloned.1.call-done = bf16[1024,512]{1,0:T(8,128)(2,1)} async-done(((bf16[128,512]{1,0:T(8,128)(2,1)}), bf16[1024,512]{1,0:T(8,128)(2,1)}) %all-gather.9.cloned.1.call-update) | async-done | bytes 1048592 | tf_op jit(solution)/shard_map/all_gather | solution.py:44
  50.0 1.5 copy.28
  51.5 4.4 %multiply_reduce_fusion.4 = (f32[128]{0:T(128)}, f32[128,512]{1,0:T(8,128)S(1)}) fusion(bf16[2,8,64,512]{3,2,1,0:T(8,128)(2,1)} %param.26, bf16[1024,8,64]{0,2,1:T(8,128)(2,1)S(1)} %bitcast.260, f32[8,128,1024]{2,1,0:T(8,128)} %copy-done.3, f32[8,128]{1,0:T(8,128)S(1)} %get-tuple-element.15, pred[128,1024]{1,0:T(8,128)(4,1)S(1)} %iota_compare_fusion, ...), kind=kOutput, calls=%fused_computation.156 | convolution fusion | flops 206045056 | bytes 6300160 | tf_op jit(solution)/shard_map/htd,hdo->to/dot_general | solution.py:50
  58.2 1.8 convolution_convert_fusion.3
  60.0 2.8 convolution_convert_fusion.2
  62.8 13.7 %all-gather.11.cloned.1.call-done = bf16[1024,512]{1,0:T(8,128)(2,1)} async-done(((bf16[128,512]{1,0:T(8,128)(2,1)}), bf16[1024,512]{1,0:T(8,128)(2,1)}) %all-gather.11.cloned.1.call-update) | async-done | bytes 1048592 | tf_op jit(solution)/shard_map/all_gather | solution.py:53
  76.5 1.5 copy.29
  78.0 13.8 %bitcast_reduce_fusion.1 = (f32[8,1024]{1,0:T(8,128)S(1)}, f32[8,1024,1024]{2,1,0:T(8,128)}) fusion(pred[1024]{0:T(1024)(128)(4,1)S(1)} %add_compare_fusion, bf16[1024,8,64]{0,2,1:T(8,128)(2,1)S(1)} %bitcast.257, bf16[1024,8,64]{0,2,1:T(8,128)(2,1)S(1)} %bitcast.253), kind=kOutput, calls=%fused_computation.5 | convolution fusion | flops 1098899456 | bytes 35685376 | tf_op jit(solution)/shard_map/tkgd,skd->kgts/dot_general | solution.py:56
  91.8 14.5 %fusion.2 = f32[8,1024]{1,0:T(8,128)S(1)} fusion(f32[8,1024,1024]{2,1,0:T(8,128)} %get-tuple-element.20, f32[8,1024]{1,0:T(8,128)S(1)} %get-tuple-element.19, pred[1024]{0:T(1024)(128)(4,1)S(1)} %add_compare_fusion), kind=kLoop, calls=%fused_computation.8 | loop fusion | flops 33546240 | bytes 33620992 | tf_op jit(solution)/shard_map/reduce_sum | solution.py:60
  106.3 23.0 %pmax.14 = f32[8,1,1024,1]{2,3,0,1:T(1,128)S(1)} all-reduce(f32[8,1,1024,1]{2,3,0,1:T(1,128)S(1)} %broadcast_in_dim.54), channel_id=1, replica_groups=mesh['dp'=2,'sp'=8] {'sp'}, use_global_device_ids=true, to_apply=%region_5.6 | all-reduce | flops 8192 | bytes 65536 | tf_op jit(solution)/shard_map/pmax | solution.py:62
  129.5 14.2 %multiply_bitcast_fusion.1 = f32[8,1,1024,64]{2,3,0,1:T(8,128)S(1)} fusion(bf16[1024,8,64]{0,2,1:T(8,128)(2,1)S(1)} %bitcast.278, f32[8,1024,1024]{2,1,0:T(8,128)} %get-tuple-element.20, f32[8,1024]{1,0:T(8,128)S(1)} %get-tuple-element.19, pred[1024]{0:T(1024)(128)(4,1)S(1)} %add_compare_fusion, f32[8,1024]{1,0:T(8,128)S(1)} %bitcast.264), kind=kOutput, calls=%fused_computation.51 | convolution fusion | flops 1107820544 | bytes 36766720 | tf_op jit(solution)/shard_map/kgts,skd->kgtd/dot_general | solution.py:61
  143.7 1.7 pad_maximum_fusion
  145.5 30.2 %reduce-scatter.3.cloned.1.call-done = f32[8,1,128,65]{2,3,0,1:T(8,128)} async-done(((f32[8,1,1024,65]{2,3,0,1:T(8,128)}), f32[8,1,128,65]{2,3,0,1:T(8,128)}) %reduce-scatter.3.cloned.1.call-update) | async-done | bytes 266256 | tf_op jit(solution)/shard_map/reduce_scatter | solution.py:64
  176.5 1.5 multiply_reduce_fusion.3
  177.9 2.1 fusion.30
  180.0 3.2 multiply_reduce_fusion.2
  183.3 1.9 convolution_convert_fusion.6
  185.4 1.9 convolution_convert_fusion.5
  187.4 1.3 convolution_convert_fusion.7
  188.8 14.9 %all-gather.13.cloned.1.call-done = bf16[1024,512]{1,0:T(8,128)(2,1)} async-done(((bf16[128,512]{1,0:T(8,128)(2,1)}), bf16[1024,512]{1,0:T(8,128)(2,1)}) %all-gather.13.cloned.1.call-update) | async-done | bytes 1048592 | tf_op jit(solution)/shard_map/all_gather | solution.py:43
  203.8 1.5 copy.32
  205.3 1.0 fusion.15
  206.3 1.9 copy-done.2
  208.2 1.7 fusion.18
  209.9 14.2 %all-gather.15.cloned.1.call-done = bf16[1024,512]{1,0:T(8,128)(2,1)} async-done(((bf16[128,512]{1,0:T(8,128)(2,1)}), bf16[1024,512]{1,0:T(8,128)(2,1)}) %all-gather.15.cloned.1.call-update) | async-done | bytes 1048592 | tf_op jit(solution)/shard_map/all_gather | solution.py:44
  224.1 1.5 copy.33
  225.6 4.4 %multiply_reduce_fusion.1 = (f32[128]{0:T(128)}, f32[128,512]{1,0:T(8,128)S(1)}) fusion(f32[128,512]{1,0:T(8,128)} %copy-done.8, bf16[2,8,64,512]{3,2,1,0:T(8,128)(2,1)} %param.26, bf16[1024,8,64]{0,2,1:T(8,128)(2,1)S(1)} %bitcast.259, f32[8,128,1024]{2,1,0:T(8,128)} %copy-done.2, f32[8,128]{1,0:T(8,128)S(1)} %get-tuple-element.25, ...), kind=kOutput, calls=%fused_computation.150 | convolution fusion | flops 205979520 | bytes 6431232 | tf_op jit(solution)/shard_map/htd,hdo->to/dot_general | solution.py:50
  232.0 1.8 convolution_convert_fusion.1
  233.8 1.8 convolution_convert_fusion
  235.6 15.1 %all-gather.17.cloned.1.call-done = bf16[1024,512]{1,0:T(8,128)(2,1)} async-done(((bf16[128,512]{1,0:T(8,128)(2,1)}), bf16[1024,512]{1,0:T(8,128)(2,1)}) %all-gather.17.cloned.1.call-update) | async-done | bytes 1048592 | tf_op jit(solution)/shard_map/all_gather | solution.py:53
  250.7 1.5 copy.34
  252.2 13.8 %bitcast_reduce_fusion = (f32[8,1024]{1,0:T(8,128)S(1)}, f32[8,1024,1024]{2,1,0:T(8,128)}) fusion(pred[1024]{0:T(1024)(128)(4,1)S(1)} %add_compare_fusion, bf16[1024,8,64]{0,2,1:T(8,128)(2,1)S(1)} %bitcast.258, bf16[1024,8,64]{0,2,1:T(8,128)(2,1)S(1)} %bitcast.254), kind=kOutput, calls=%fused_computation.1 | convolution fusion | flops 1098899456 | bytes 35685376 | tf_op jit(solution)/shard_map/tkgd,skd->kgts/dot_general | solution.py:56
  266.0 14.5 %fusion.4 = f32[8,1024]{1,0:T(8,128)S(1)} fusion(f32[8,1024,1024]{2,1,0:T(8,128)} %get-tuple-element.30, f32[8,1024]{1,0:T(8,128)S(1)} %get-tuple-element.29, pred[1024]{0:T(1024)(128)(4,1)S(1)} %add_compare_fusion), kind=kLoop, calls=%fused_computation.10 | loop fusion | flops 33546240 | bytes 33620992 | tf_op jit(solution)/shard_map/reduce_sum | solution.py:60
  280.4 22.9 %pmax.15 = f32[8,1,1024,1]{2,3,0,1:T(1,128)S(1)} all-reduce(f32[8,1,1024,1]{2,3,0,1:T(1,128)S(1)} %broadcast_in_dim.56), channel_id=1, replica_groups=mesh['dp'=2,'sp'=8] {'sp'}, use_global_device_ids=true, to_apply=%region_14.15 | all-reduce | flops 8192 | bytes 65536 | tf_op jit(solution)/shard_map/pmax | solution.py:62
  303.5 14.2 %multiply_bitcast_fusion = f32[8,1,1024,64]{2,3,0,1:T(8,128)S(1)} fusion(bf16[1024,8,64]{0,2,1:T(8,128)(2,1)S(1)} %bitcast.277, f32[8,1024,1024]{2,1,0:T(8,128)} %get-tuple-element.30, f32[8,1024]{1,0:T(8,128)S(1)} %get-tuple-element.29, pred[1024]{0:T(1024)(128)(4,1)S(1)} %add_compare_fusion, f32[8,1024]{1,0:T(8,128)S(1)} %bitcast.263), kind=kOutput, calls=%fused_computation.47 | convolution fusion | flops 1107820544 | bytes 36766720 | tf_op jit(solution)/shard_map/kgts,skd->kgtd/dot_general | solution.py:61
  317.7 1.7 pad_maximum_fusion.1
  319.4 30.3 %reduce-scatter.5.cloned.1.call-done = f32[8,1,128,65]{2,3,0,1:T(8,128)} async-done(((f32[8,1,1024,65]{2,3,0,1:T(8,128)}), f32[8,1,128,65]{2,3,0,1:T(8,128)}) %reduce-scatter.5.cloned.1.call-update) | async-done | bytes 266256 | tf_op jit(solution)/shard_map/reduce_scatter | solution.py:64
  350.5 1.3 multiply_reduce_fusion
  351.8 2.2 fusion.25
  354.0 3.8 %fusion.66 = bf16[128,512]{1,0:T(8,128)(2,1)} fusion(f32[128,512]{1,0:T(8,128)S(1)} %get-tuple-element.32, bf16[2,2048,512]{2,1,0:T(8,128)(2,1)} %param.33, bf16[2,512,2048]{2,1,0:T(8,128)(2,1)} %param.32, f32[128,2048]{1,0:T(8,128)S(1)} %fusion.25, f32[512]{0:T(512)S(1)} %bitcast.268, f32[128]{0:T(128)S(1)} %add_rsqrt_fusion), kind=kOutput, calls=%fused_computation.78 | convolution fusion | flops 538771456 | bytes 5900800 | tf_op jit(solution)/shard_map/dot_general | solution.py:73
  (64 shorter events, 9.1 us)
Async XLA Ops:
  6.5 51.7 %copy-start = (bf16[1024,512]{1,0:T(8,128)(2,1)S(1)}, bf16[1024,512]{1,0:T(8,128)(2,1)}, u32[]{:S(2)}) copy-start(bf16[1024,512]{1,0:T(8,128)(2,1)} %param.18) | copy-start | bytes 3145732
  6.6 22.9 %all-gather.7.cloned.1.call-start = ((), (), s32[]{:S(2)}) async-start(), calls=%async_computation.2 | async-start | bytes 1179648 | tf_op jit(solution)/shard_map/all_gather | solution.py:43
  10.5 39.5 %all-gather.9.cloned.1.call-start = ((), (), s32[]{:S(2)}) async-start(), calls=%async_computation.3 | async-start | bytes 1179648 | tf_op jit(solution)/shard_map/all_gather | solution.py:44
  12.7 63.8 %all-gather.11.cloned.1.call-start = ((), (), s32[]{:S(2)}) async-start(), calls=%async_computation.4 | async-start | bytes 1179648 | tf_op jit(solution)/shard_map/all_gather | solution.py:53
  31.9 1.9 copy-start.3
  51.5 5.0 %copy-start.4 = (bf16[2,512,512]{2,1,0:T(8,128)(2,1)S(1)}, bf16[2,512,512]{2,1,0:T(8,128)(2,1)}, u32[]{:S(2)}) copy-start(bf16[2,512,512]{2,1,0:T(8,128)(2,1)} %param.27) | copy-start | bytes 3145732
  55.8 22.2 %copy-start.6 = (f32[128,512]{1,0:T(8,128)}, f32[128,512]{1,0:T(8,128)S(1)}, u32[]{:S(2)}) copy-start(f32[128,512]{1,0:T(8,128)S(1)} %get-tuple-element.18) | copy-start | bytes 786436
  57.5 118.2 %reduce-scatter.3.cloned.1.call-start = ((), (), s32[]{:S(2)}) async-start(), calls=%async_computation.5 | async-start | bytes 2654208 | tf_op jit(solution)/shard_map/reduce_scatter | solution.py:64
  91.8 37.6 %copy-start.11 = (bf16[1024,512]{0,1:T(8,128)(2,1)S(1)}, bf16[1024,512]{0,1:T(8,128)(2,1)}, u32[]{:S(2)}) copy-start(bf16[1024,512]{0,1:T(8,128)(2,1)} %convolution_convert_fusion.2) | copy-start | bytes 3145732
  143.6 1.9 copy-start.9
  143.6 32.8 %copy-start.7 = (f32[128,512]{1,0:T(8,128)S(1)}, f32[128,512]{1,0:T(8,128)}, u32[]{:S(2)}) copy-start(f32[128,512]{1,0:T(8,128)} %copy-done.6) | copy-start | bytes 786436
  145.4 58.3 %all-gather.13.cloned.1.call-start = ((), (), s32[]{:S(2)}) async-start(), calls=%async_computation.6 | async-start | bytes 1179648 | tf_op jit(solution)/shard_map/all_gather | solution.py:43
  183.2 23.0 %copy-start.8 = (f32[128,512]{1,0:T(8,128)}, f32[128,512]{1,0:T(8,128)S(1)}, u32[]{:S(2)}) copy-start(f32[128,512]{1,0:T(8,128)S(1)} %get-tuple-element.24) | copy-start | bytes 786436
  185.3 38.8 %all-gather.15.cloned.1.call-start = ((), (), s32[]{:S(2)}) async-start(), calls=%async_computation.7 | async-start | bytes 1179648 | tf_op jit(solution)/shard_map/all_gather | solution.py:44
  187.4 63.3 %all-gather.17.cloned.1.call-start = ((), (), s32[]{:S(2)}) async-start(), calls=%async_computation.8 | async-start | bytes 1179648 | tf_op jit(solution)/shard_map/all_gather | solution.py:53
  206.2 1.9 copy-start.2
  225.6 5.1 %copy-start.5 = (bf16[2,512,512]{2,1,0:T(8,128)(2,1)S(1)}, bf16[2,512,512]{2,1,0:T(8,128)(2,1)}, u32[]{:S(2)}) copy-start(bf16[2,512,512]{2,1,0:T(8,128)(2,1)} %param.27) | copy-start | bytes 3145732
  231.7 118.0 %reduce-scatter.5.cloned.1.call-start = ((), (), s32[]{:S(2)}) async-start(), calls=%async_computation.9 | async-start | bytes 2654208 | tf_op jit(solution)/shard_map/reduce_scatter | solution.py:64
  317.7 32.8 %copy-start.10 = (bf16[2,8,64,512]{3,2,1,0:T(8,128)(2,1)S(1)}, bf16[2,8,64,512]{3,2,1,0:T(8,128)(2,1)}, u32[]{:S(2)}) copy-start(bf16[2,8,64,512]{3,2,1,0:T(8,128)(2,1)} %param.30) | copy-start | bytes 3145732
  351.8 5.9 %copy-start.1 = (bf16[1024,512]{1,0:T(8,128)(2,1)S(1)}, bf16[1024,512]{1,0:T(8,128)(2,1)}, u32[]{:S(2)}) copy-start(bf16[1024,512]{1,0:T(8,128)(2,1)} %param.18) | copy-start | bytes 3145732
Sparse Core Ops, SparseCore 0:
  10.6 18.8 all-gather.6
  31.1 18.8 all-gather.8
  57.6 18.8 all-gather.10
  145.5 30.1 reduce-scatter.2
  185.4 18.2 all-gather.12
  205.2 18.8 all-gather.14
  231.8 18.8 all-gather.16
  319.6 30.1 reduce-scatter.4
where the time goes:
time: 369 us; the launch traced here: 365 us
  waiting for transfers between devices  148 us (40%)
  matrix products  101 us (27%)
  blocking collectives  45.9 us (12%)
  other arithmetic  40.1 us (11%)
  local copies, waits for them, and re-layouts  14.6 us (4%)
  between operations  14.6 us (4%)
    reduce_scatter x2, waiting for transfers between devices, local_step(): combined = lax.psum_scatter(packed, 'sp', scatter_dimension=2, tiled=True)  60.4 us
    pmax x2, blocking collectives, local_step(): rescale = jnp.exp(part_max - lax.pmax(part_max, 'sp'))  45.9 us
    all_gather x2, waiting for transfers between devices, local_step(): lax.all_gather(project(normed, self_k[layer]), 'sp', axis=0, tiled=True)  29.2 us
    reduce_sum x2, other arithmetic, local_step(): part_sum = jnp.sum(weights, axis=-1, keepdims=True)  29 us
    all_gather x2, waiting for transfers between devices, local_step(): lax.all_gather(project(normed, cross_q[layer]), 'sp', axis=0, tiled=True)  28.8 us
    all_gather x2, waiting for transfers between devices, local_step(): lax.all_gather(project(normed, self_v[layer]), 'sp', axis=0, tiled=True)  28.7 us
    dot_general x2, matrix products, local_step(): jnp.einsum('kgts,skd->kgtd', weights.astype(jnp.bfloat16), mem_values, pr...  28.3 us
    dot_general x2, matrix products, local_step(): jnp.einsum('tkgd,skd->kgts', cross_queries, mem_keys, preferred_element_t...  27.5 us
  transfers between devices with their start and end apart: 8, of which 8 were waited for; matrix products, arithmetic and copies ran while one was open for 7% of the time, Pallas kernels for 0%

commit v1 on v0

v1 whole, which is shorter than its diff:
```python
import functools

import jax
import jax.numpy as jnp
from jax import lax
from jax.experimental import pallas as pl
from jax.experimental.pallas import tpu as pltpu
from jax.sharding import PartitionSpec as P

EPS = 1e-6
NEG_BIG = -1e30
CORES = 2
KEY_BLOCK = 512
FF_BLOCK = 512
MEM_BLOCK = 256
F32 = jnp.float32
BF16 = jnp.bfloat16
MESH = pl.DeviceIdType.MESH
WEIGHTS = ('self_q', 'self_k', 'self_v', 'self_o', 'cross_k', 'cross_v', 'cross_q', 'cross_o', 'mlp_gate', 'mlp_up', 'mlp_down')
HALVED = ('cross_k', 'cross_v')


def rms_norm(hidden, gain_row):
    hidden32 = hidden.astype(F32)
    inv_rms = lax.rsqrt(jnp.mean(hidden32 * hidden32, axis=-1, keepdims=True) + EPS)
    return (hidden32 * inv_rms * gain_row.astype(F32)).astype(BF16)


def mm(a, b):
    return jnp.dot(a, b, preferred_element_type=F32)


def mm_t(a, b):
    return lax.dot_general(a, b, (((1,), (1,)), ((), ())), preferred_element_type=F32)


def lane_groups(rows, lanes, head_dim):
    return lax.broadcasted_iota(jnp.int32, (rows, lanes), 1) // head_dim


def stack_heads(q, head_dim, scale):
    rows, lanes = q.shape
    scaled = q.astype(F32) * scale
    group = lane_groups(rows, lanes, head_dim)
    return jnp.concatenate([jnp.where(group == h, scaled, 0.0).astype(BF16) for h in range(lanes // head_dim)], axis=0)


def attend(q_stack, key_block, value_block, n_keys, allowed, scores_ref):
    rows = q_stack.shape[0]
    run_max = None
    for start in range(0, n_keys, KEY_BLOCK):
        scores = mm_t(q_stack, key_block(start))
        scores = jnp.where(allowed(start), scores, NEG_BIG)
        scores_ref[:, start:start + KEY_BLOCK] = scores
        for lane in range(0, KEY_BLOCK, 128):
            tile = scores[:, lane:lane + 128]
            run_max = tile if run_max is None else jnp.maximum(run_max, tile)
    top = jnp.max(run_max, axis=-1, keepdims=True)
    run_sum = None
    numerator = None
    for start in range(0, n_keys, KEY_BLOCK):
        weights = jnp.exp(scores_ref[:, start:start + KEY_BLOCK] - top)
        for lane in range(0, KEY_BLOCK, 128):
            tile = weights[:, lane:lane + 128]
            run_sum = tile if run_sum is None else run_sum + tile
        part = mm(weights.astype(BF16), value_block(start))
        numerator = part if numerator is None else numerator + part
    return numerator, top, jnp.sum(run_sum, axis=-1, keepdims=True)


def unstack_heads(stacked, rows, head_dim):
    lanes = stacked.shape[1]
    group = lane_groups(rows, lanes, head_dim)
    out = stacked[:rows]
    for h in range(1, lanes // head_dim):
        out = jnp.where(group == h, stacked[h * rows:(h + 1) * rows], out)
    return out


def kernel(group, n_layers, head_dim, *refs):
    n_w = len(WEIGHTS)
    hidden_ref, memory_ref, mem_len_ref, norm_self, norm_cross, norm_mlp = refs[:6]
    w_hbm = dict(zip(WEIGHTS, refs[6:6 + n_w]))
    out_ref = refs[6 + n_w]
    scratch = refs[7 + n_w:]
    w = dict(zip(WEIGHTS, scratch[:n_w]))
    (mem_v, x_all, k_all, v_all, mem_k, mem_vals, q_send, q_all, part_send, part_recv, stat_send, stat_recv, hid, scores_ref,
     w_sem, mem_sem, mem_send, mem_recv, x_send, x_relay, x_recv, q_ssem, q_rsem, p_ssem, p_rsem, s_ssem, s_rsem) = scratch[n_w:]

    rows, width = hidden_ref.shape
    mem_rows = memory_ref.shape[0]
    chips = group // CORES
    half = q_send.shape[-1]
    hpg = half // head_dim
    scale = head_dim ** -0.5
    me = lax.axis_index('sp')
    chip, core = me // CORES, me % CORES
    partner = chip * CORES + (1 - core)

    def remote(src, dst, ssem, rsem, dev):
        return pltpu.make_async_remote_copy(src_ref=src, dst_ref=dst, send_sem=ssem, recv_sem=rsem, device_id={'sp': dev}, device_id_type=MESH)

    def weight_copy(name, layer):
        src = w_hbm[name].at[layer]
        if name in HALVED:
            src = w_hbm[name].at[layer, :, pl.ds(pl.multiple_of(core * half, half), half)]
        return pltpu.make_async_copy(src, w[name].at[layer], w_sem.at[WEIGHTS.index(name), layer])

    mem_copy = pltpu.make_async_copy(memory_ref, mem_v.at[core], mem_sem.at[0])

    for name in ('self_q', 'self_k', 'self_v'):
        weight_copy(name, 0).start()
    mem_copy.start()
    for layer in range(n_layers):
        for name in HALVED:
            weight_copy(name, layer).start()
    for layer in range(n_layers):
        for name in WEIGHTS:
            if name in HALVED or (layer == 0 and name in ('self_q', 'self_k', 'self_v')):
                continue
            weight_copy(name, layer).start()

    barrier = pltpu.get_barrier_semaphore()
    for step in range(1, group):
        pl.semaphore_signal(barrier, inc=1, device_id={'sp': lax.rem(me + step, group)}, device_id_type=MESH)
    pl.semaphore_wait(barrier, group - 1)

    def x_to_chip(layer, d):
        return remote(x_all.at[layer, me], x_all.at[layer, me], x_send.at[layer, d], x_recv.at[layer, me], me + d * CORES)

    def x_to_partner(layer):
        return remote(x_all.at[layer, me], x_all.at[layer, me], x_send.at[layer, 0], x_recv.at[layer, me], partner)

    def x_relayed(layer, d):
        src = me - d * CORES
        return remote(x_all.at[layer, src], x_all.at[layer, src], x_relay.at[layer, d], x_recv.at[layer, src], partner)

    def x_arrival(layer, src):
        return remote(x_all.at[layer, src], x_all.at[layer, src], x_send.at[layer, 0], x_recv.at[layer, src], partner)

    def q_copy(layer, d, k):
        dst = lax.rem(chip + d, chips) * CORES + k
        return remote(q_send.at[layer, k], q_all.at[layer, me], q_ssem.at[layer, d * CORES + k], q_rsem.at[layer, me], dst)

    def q_to_partner(layer):
        return remote(q_send.at[layer, 1 - core], q_all.at[layer, me], q_ssem.at[layer, 0], q_rsem.at[layer, me], partner)

    def q_arrival(layer, src):
        return remote(q_send.at[layer, 0], q_all.at[layer, src], q_ssem.at[layer, 0], q_rsem.at[layer, src], partner)

    def part_copy(layer, src):
        return remote(part_send.at[layer, src], part_recv.at[layer, me], p_ssem.at[layer, src], p_rsem.at[layer, me], src)

    def stat_copy(layer, src):
        return remote(stat_send.at[layer, src], stat_recv.at[layer, me], s_ssem.at[layer, src], s_rsem.at[layer, me], src)

    def part_arrival(layer, src):
        return remote(part_send.at[layer, src], part_recv.at[layer, src], p_ssem.at[layer, src], p_rsem.at[layer, src], partner)

    def stat_arrival(layer, src):
        return remote(stat_send.at[layer, src], stat_recv.at[layer, src], s_ssem.at[layer, src], s_rsem.at[layer, src], partner)

    mem_out = remote(mem_v.at[core], mem_v.at[core], mem_send.at[0], mem_recv.at[0], partner)
    mem_in = remote(mem_v.at[1 - core], mem_v.at[1 - core], mem_send.at[0], mem_recv.at[0], partner)

    def project_memory(slot):
        def body(i, carry):
            at = pl.ds(pl.multiple_of(i * MEM_BLOCK, MEM_BLOCK), MEM_BLOCK)
            to = pl.ds(pl.multiple_of(slot * mem_rows + i * MEM_BLOCK, MEM_BLOCK), MEM_BLOCK)
            block = mem_v[slot, at, :]
            for layer in range(n_layers):
                mem_k[layer, to, :] = mm(block, w['cross_k'][layer]).astype(BF16)
                mem_vals[layer, to, :] = mm(block, w['cross_v'][layer]).astype(BF16)
            return carry
        lax.fori_loop(0, mem_rows // MEM_BLOCK, body, 0)

    hid[...] = hidden_ref[...]
    for src in range(group):
        @pl.when(src > me)
        def _():
            k_all[src] = jnp.zeros((rows, width), BF16)
            v_all[src] = jnp.zeros((rows, width), BF16)

    for layer in range(n_layers):
        x_all[layer, me] = rms_norm(hid[...], norm_self[layer:layer + 1, :])
        for d in (2, 1, 3):
            if d < chips:
                @pl.when(chip + d < chips)
                def _():
                    x_to_chip(layer, d).start()

        @pl.when(core == 0)
        def _():
            x_to_partner(layer).start()

        if layer == 0:
            for name in ('self_q', 'self_k', 'self_v'):
                weight_copy(name, layer).wait()
        else:
            for name in ('self_q', 'self_k', 'self_v'):
                weight_copy(name, layer).wait()

        def project_rows(src):
            block = x_all[layer, src]
            k_all[src] = mm(block, w['self_k'][layer]).astype(BF16)
            v_all[src] = mm(block, w['self_v'][layer]).astype(BF16)

        project_rows(me)
        queries = mm(x_all[layer, me], w['self_q'][layer]).astype(BF16)

        if layer == 0:
            mem_copy.wait()
            mem_out.start()
            for other in range(n_layers):
                for name in HALVED:
                    weight_copy(name, other).wait()
            project_memory(core)

        for d in range(1, chips):
            @pl.when(chip - d >= 0)
            def _():
                x_arrival(layer, me - d * CORES).wait_recv()
                x_relayed(layer, d).start()
                project_rows(me - d * CORES)

        @pl.when(core == 1)
        def _():
            x_arrival(layer, partner).wait_recv()
            project_rows(partner)

        for d in range(1, chips):
            @pl.when(chip - d >= 0)
            def _():
                x_arrival(layer, partner - d * CORES).wait_recv()
                project_rows(partner - d * CORES)

        if layer == 0:
            mem_in.wait_recv()
            project_memory(1 - core)

        all_rows = group * rows
        query_at = me * rows + lax.rem(lax.broadcasted_iota(jnp.int32, (hpg * rows, KEY_BLOCK), 0), rows)
        key_at = lax.broadcasted_iota(jnp.int32, (hpg * rows, KEY_BLOCK), 1)
        per_block = KEY_BLOCK // rows
        attended = []
        for g in range(CORES):
            lanes = slice(g * half, (g + 1) * half)
            num, _, den = attend(
                stack_heads(queries[:, lanes], head_dim, scale),
                lambda start: k_all[start // rows:start // rows + per_block, :, lanes].reshape(KEY_BLOCK, half),
                lambda start: v_all[start // rows:start // rows + per_block, :, lanes].reshape(KEY_BLOCK, half),
                all_rows, lambda start: key_at + start <= query_at, scores_ref)
            attended.append(unstack_heads(num / den, rows, head_dim).astype(BF16))
        attended = jnp.concatenate(attended, axis=-1)
        weight_copy('self_o', layer).wait()
        hidden = (hid[...].astype(F32) + mm(attended, w['self_o'][layer])).astype(BF16)
        hid[...] = hidden

        weight_copy('cross_q', layer).wait()
        queries = mm(rms_norm(hidden, norm_cross[layer:layer + 1, :]), w['cross_q'][layer]).astype(BF16)
        for g in range(CORES):
            q_send[layer, g] = queries[:, g * half:(g + 1) * half]
        q_to_partner(layer).start()
        for d in (1, 3, 2):
            if d < chips:
                for k in range(CORES):
                    q_copy(layer, d, k).start()
        q_all[layer, me] = q_send[layer, core]

        mem_at = chip * (CORES * mem_rows) + lax.broadcasted_iota(jnp.int32, (1, KEY_BLOCK), 1)
        last = group - 1

        def chunk(j, carry):
            is_last = j // last
            is_first = 1 - (j + last - 1) // last
            mid = 1 - is_first - is_last
            pair = (j + 1) // CORES - 1
            d = mid * (1 + CORES * pair - 3 * (pair // 2))
            k = is_first * core + is_last * (1 - core) + mid * lax.rem(j + 1, CORES)
            src = lax.rem(chip + d, chips) * CORES + k

            @pl.when(j > 0)
            def _():
                q_arrival(layer, src).wait_recv()

            num, top, den = attend(
                stack_heads(q_all[layer, src], head_dim, scale),
                lambda start: mem_k[layer, start:start + KEY_BLOCK, :],
                lambda start: mem_vals[layer, start:start + KEY_BLOCK, :],
                CORES * mem_rows, lambda start: mem_at + start < mem_len_ref[0], scores_ref)
            part = unstack_heads(num, rows, head_dim).astype(BF16)
            lane = lax.broadcasted_iota(jnp.int32, (rows, 128), 1)
            stats = jnp.zeros((rows, 128), F32)
            for h in range(hpg):
                stats = jnp.where(lane == h, top[h * rows:(h + 1) * rows], stats)
                stats = jnp.where(lane == hpg + h, den[h * rows:(h + 1) * rows], stats)
            stats = jnp.transpose(stats)[:2 * hpg]

            @pl.when(j == 0)
            def _():
                part_recv[layer, me] = part
                stat_recv[layer, me] = stats

            @pl.when(j > 0)
            def _():
                part_send[layer, src] = part
                stat_send[layer, src] = stats
                part_copy(layer, src).start()
                stat_copy(layer, src).start()
            return carry

        lax.fori_loop(0, group, chunk, 0)

        def arrived(step, carry):
            src = lax.rem(me + step, group)
            stat_arrival(layer, src).wait_recv()
            part_arrival(layer, src).wait_recv()
            return carry

        lax.fori_loop(1, group, arrived, 0)

        factors = [None] * group
        for g in range(CORES):
            members = [c * CORES + g for c in range(chips)]
            tops = [stat_recv[layer, i, 0:hpg] for i in members]
            dens = [stat_recv[layer, i, hpg:2 * hpg] for i in members]
            best = functools.reduce(jnp.maximum, tops)
            shares = [jnp.exp(t - best) for t in tops]
            total = functools.reduce(jnp.add, [s * d for s, d in zip(shares, dens)])
            for i, s in zip(members, shares):
                factors[i] = s / total
        packed = jnp.concatenate(factors + [jnp.zeros((128 - group * hpg, rows), F32)], axis=0)
        packed = jnp.transpose(packed)
        lane_group = lane_groups(rows, half, head_dim)
        attended = []
        for g in range(CORES):
            total = jnp.zeros((rows, half), F32)
            for c in range(chips):
                i = c * CORES + g
                factor = jnp.zeros((rows, half), F32)
                for h in range(hpg):
                    factor = jnp.where(lane_group == h, packed[:, i * hpg + h:i * hpg + h + 1], factor)
                total = total + part_recv[layer, i].astype(F32) * factor
            attended.append(total.astype(BF16))
        attended = jnp.concatenate(attended, axis=-1)
        weight_copy('cross_o', layer).wait()
        hidden = (hid[...].astype(F32) + mm(attended, w['cross_o'][layer])).astype(BF16)

        normed = rms_norm(hidden, norm_mlp[layer:layer + 1, :])
        for name in ('mlp_gate', 'mlp_up', 'mlp_down'):
            weight_copy(name, layer).wait()
        update = None
        for start in range(0, w['mlp_gate'].shape[-1], FF_BLOCK):
            cols = slice(start, start + FF_BLOCK)
            gate = mm(normed, w['mlp_gate'][layer, :, cols])
            up = mm(normed, w['mlp_up'][layer, :, cols])
            act = (gate * jax.nn.sigmoid(gate) * up).astype(BF16)
            part = mm(act, w['mlp_down'][layer, cols, :])
            update = part if update is None else update + part
        hidden = (hidden.astype(F32) + update).astype(BF16)
        hid[...] = hidden

    out_ref[...] = hid[...]

    mem_out.wait_send()
    for layer in range(n_layers):
        for d in range(1, chips):
            @pl.when(chip + d < chips)
            def _():
                x_to_chip(layer, d).wait_send()

            @pl.when(chip - d >= 0)
            def _():
                x_relayed(layer, d).wait_send()

            for k in range(CORES):
                q_copy(layer, d, k).wait_send()

        @pl.when(core == 0)
        def _():
            x_to_partner(layer).wait_send()
        q_to_partner(layer).wait_send()

        def sent(step, carry):
            src = lax.rem(me + step, group)
            part_copy(layer, src).wait_send()
            stat_copy(layer, src).wait_send()
            return carry

        lax.fori_loop(1, group, sent, 0)


def solution(mesh):
    group = mesh.shape['sp']
    row_spec = P(('dp', 'sp'), None)

    def local_step(hidden, memory, mem_len, norm_self, norm_cross, norm_mlp, self_q, self_k, self_v, self_o, cross_q, cross_k, cross_v, cross_o, mlp_gate, mlp_up, mlp_down):
        rows, width = hidden.shape
        mem_rows = memory.shape[0]
        n_layers, n_heads, head_dim = self_o.shape[:3]
        inner = n_heads * head_dim
        half = inner // CORES
        hpg = half // head_dim
        all_keys = max(group * rows, CORES * mem_rows)
        weights = dict(
            self_q=self_q, self_k=self_k, self_v=self_v, self_o=self_o.reshape(n_layers, inner, width), cross_k=cross_k, cross_v=cross_v,
            cross_q=cross_q, cross_o=cross_o.reshape(n_layers, inner, width), mlp_gate=mlp_gate, mlp_up=mlp_up, mlp_down=mlp_down)
        w_scratch = [
            pltpu.VMEM((n_layers, width, half) if name in HALVED else weights[name].shape, BF16) for name in WEIGHTS]
        dma = pltpu.SemaphoreType.DMA
        vmem = pl.BlockSpec(memory_space=pltpu.VMEM)
        hbm = pl.BlockSpec(memory_space=pl.ANY)
        return pl.pallas_call(
            functools.partial(kernel, group, n_layers, head_dim),
            out_shape=jax.ShapeDtypeStruct((rows, width), BF16),
            in_specs=[vmem, hbm, pl.BlockSpec(memory_space=pltpu.SMEM), vmem, vmem, vmem] + [hbm] * len(WEIGHTS),
            out_specs=vmem,
            scratch_shapes=w_scratch + [
                pltpu.VMEM((CORES, mem_rows, width), BF16),
                pltpu.VMEM((n_layers, group, rows, width), BF16),
                pltpu.VMEM((group, rows, width), BF16),
                pltpu.VMEM((group, rows, width), BF16),
                pltpu.VMEM((n_layers, CORES * mem_rows, half), BF16),
                pltpu.VMEM((n_layers, CORES * mem_rows, half), BF16),
                pltpu.VMEM((n_layers, CORES, rows, half), BF16),
                pltpu.VMEM((n_layers, group, rows, half), BF16),
                pltpu.VMEM((n_layers, group, rows, half), BF16),
                pltpu.VMEM((n_layers, group, rows, half), BF16),
                pltpu.VMEM((n_layers, group, 2 * hpg, rows), F32),
                pltpu.VMEM((n_layers, group, 2 * hpg, rows), F32),
                pltpu.VMEM((rows, width), BF16),
                pltpu.VMEM((hpg * rows, all_keys), F32),
                dma((len(WEIGHTS), n_layers)),
                dma((1,)), dma((1,)), dma((1,)),
                dma((n_layers, group // CORES)), dma((n_layers, group // CORES)), dma((n_layers, group)),
                dma((n_layers, group)), dma((n_layers, group)),
                dma((n_layers, group)), dma((n_layers, group)),
                dma((n_layers, group)), dma((n_layers, group)),
            ],
            compiler_params=pltpu.CompilerParams(collective_id=0, has_side_effects=True, vmem_limit_bytes=60 * 1024 * 1024),
        )(hidden, memory, mem_len, norm_self, norm_cross, norm_mlp, *[weights[name] for name in WEIGHTS])

    return jax.shard_map(local_step, mesh=mesh, in_specs=(row_spec, row_spec, P('dp')) + (P(),) * 14, out_specs=row_spec, check_vma=False)
```

time: 369 us -> 93.8 us (0.25)
  the two profiles are of different devices: /device:TPU:127 before, /device:TPU:112 now
where the time goes in v1:
time: 93.8 us; the launch traced here: 93.6 us
  Pallas kernels  91.4 us (97%)
  local copies, waits for them, and re-layouts  1.57 us (2%)
    pallas_call x1, Pallas kernels, local_step(): pl.pallas_call(functools.partial(kernel, group, n_layers, head_dim), out_...  91.4 us

profile of v1, /device:TPU:112, one launch (start us, length us, event | category | flops | bytes accessed | tf_op | source)
XLA Modules:
  0.0 93.6 jit_solution(4598252987208832307)
XLA Ops:
  0.7 91.4 %shard_map.163 = bf16[128,512]{1,0:T(8,128)(2,1)} custom-call(bf16[128,512]{1,0:T(8,128)(2,1)} %refs_0_.1, bf16[1024,512]{1,0:T(8,128)(2,1)} %refs_1_.1, s32[1]{0:T(128)S(6)} %copy.19.refs_2_, bf16[2,512]{1,0:T(2,128)(2,1)} %refs_3_.1, bf16[2,512]{1,0:T(2,128)(2,1)} %refs_4_.1, bf16[2,512]{1,0:T(2,128)(2,1)} %refs_5_.1, bf16[2,512,512]{2,1,0:T(8,128)(2,1)} %refs_6_.1, ...), custom_call_target="tpu_custom_call" | custom-call | tf_op jit(solution)/shard_map/pallas_call | solution.py:413
  92.1 1.6 %copy.20 = bf16[128,512]{1,0:T(8,128)(2,1)} copy(bf16[128,512]{1,0:T(8,128)(2,1)} %shard_map.163) | data formatting | bytes 262144

commit v2 on v1

--- a/solution.py
+++ b/solution.py
@@ -13,6 +13,7 @@
 KEY_BLOCK = 512
 FF_BLOCK = 512
 MEM_BLOCK = 256
+MEM_LEN_MAX = 6144
 F32 = jnp.float32
 BF16 = jnp.bfloat16
 MESH = pl.DeviceIdType.MESH
@@ -45,8 +46,7 @@
     return jnp.concatenate([jnp.where(group == h, scaled, 0.0).astype(BF16) for h in range(lanes // head_dim)], axis=0)
 
 
-def attend(q_stack, key_block, value_block, n_keys, allowed, scores_ref):
-    rows = q_stack.shape[0]
+def score(q_stack, key_block, n_keys, allowed, scores_ref, max_ref):
     run_max = None
     for start in range(0, n_keys, KEY_BLOCK):
         scores = mm_t(q_stack, key_block(start))
@@ -55,7 +55,11 @@
         for lane in range(0, KEY_BLOCK, 128):
             tile = scores[:, lane:lane + 128]
             run_max = tile if run_max is None else jnp.maximum(run_max, tile)
-    top = jnp.max(run_max, axis=-1, keepdims=True)
+    max_ref[...] = run_max
+
+
+def gather_values(value_block, n_keys, scores_ref, max_ref):
+    top = jnp.max(max_ref[...], axis=-1, keepdims=True)
     run_sum = None
     numerator = None
     for start in range(0, n_keys, KEY_BLOCK):
@@ -77,6 +81,18 @@
     return out
 
 
+class Phase:
+    def __init__(self):
+        self.cur = None
+
+    def __call__(self, name):
+        if self.cur is not None:
+            self.cur.__exit__(None, None, None)
+        self.cur = jax.named_scope(name) if name else None
+        if self.cur is not None:
+            self.cur.__enter__()
+
+
 def kernel(group, n_layers, head_dim, *refs):
     n_w = len(WEIGHTS)
     hidden_ref, memory_ref, mem_len_ref, norm_self, norm_cross, norm_mlp = refs[:6]
@@ -84,12 +100,13 @@
     out_ref = refs[6 + n_w]
     scratch = refs[7 + n_w:]
     w = dict(zip(WEIGHTS, scratch[:n_w]))
-    (mem_v, x_all, k_all, v_all, mem_k, mem_vals, q_send, q_all, part_send, part_recv, stat_send, stat_recv, hid, scores_ref,
+    (mem_v, x_all, k_all, v_all, mem_k, mem_vals, q_send, q_all, part_send, part_recv, stat_send, stat_recv, hid, scores_a, scores_b, max_a, max_b,
      w_sem, mem_sem, mem_send, mem_recv, x_send, x_relay, x_recv, q_ssem, q_rsem, p_ssem, p_rsem, s_ssem, s_rsem) = scratch[n_w:]
 
     rows, width = hidden_ref.shape
     mem_rows = memory_ref.shape[0]
     chips = group // CORES
+    mem_chips = -(-MEM_LEN_MAX // (CORES * mem_rows))
     half = q_send.shape[-1]
     hpg = half // head_dim
     scale = head_dim ** -0.5
@@ -106,6 +123,8 @@
             src = w_hbm[name].at[layer, :, pl.ds(pl.multiple_of(core * half, half), half)]
         return pltpu.make_async_copy(src, w[name].at[layer], w_sem.at[WEIGHTS.index(name), layer])
 
+    phase = Phase()
+    phase('start')
     mem_copy = pltpu.make_async_copy(memory_ref, mem_v.at[core], mem_sem.at[0])
 
     for name in ('self_q', 'self_k', 'self_v'):
@@ -120,6 +139,7 @@
                 continue
             weight_copy(name, layer).start()
 
+    phase('barrier')
     barrier = pltpu.get_barrier_semaphore()
     for step in range(1, group):
         pl.semaphore_signal(barrier, inc=1, device_id={'sp': lax.rem(me + step, group)}, device_id_type=MESH)
@@ -174,6 +194,7 @@
             return carry
         lax.fori_loop(0, mem_rows // MEM_BLOCK, body, 0)
 
+    phase('zero')
     hid[...] = hidden_ref[...]
     for src in range(group):
         @pl.when(src > me)
@@ -182,6 +203,7 @@
             v_all[src] = jnp.zeros((rows, width), BF16)
 
     for layer in range(n_layers):
+        phase(f'xnorm{layer}')
         x_all[layer, me] = rms_norm(hid[...], norm_self[layer:layer + 1, :])
         for d in (2, 1, 3):
             if d < chips:
@@ -205,16 +227,22 @@
             k_all[src] = mm(block, w['self_k'][layer]).astype(BF16)
             v_all[src] = mm(block, w['self_v'][layer]).astype(BF16)
 
+        phase(f'ownproj{layer}')
         project_rows(me)
         queries = mm(x_all[layer, me], w['self_q'][layer]).astype(BF16)
 
+        phase(f'memproj{layer}')
         if layer == 0:
             mem_copy.wait()
-            mem_out.start()
             for other in range(n_layers):
                 for name in HALVED:
                     weight_copy(name, other).wait()
-            project_memory(core)
+
+            @pl.when(chip < mem_chips)
+            def _():
+                mem_out.start()
+                project_memory(core)
+        phase(f'xwait{layer}')
 
         for d in range(1, chips):
             @pl.when(chip - d >= 0)
@@ -234,94 +262,122 @@
                 x_arrival(layer, partner - d * CORES).wait_recv()
                 project_rows(partner - d * CORES)
 
+        phase(f'memproj2{layer}')
         if layer == 0:
-            mem_in.wait_recv()
-            project_memory(1 - core)
-
+            @pl.when(chip < mem_chips)
+            def _():
+                mem_in.wait_recv()
+                project_memory(1 - core)
+
+        phase(f'selfatt{layer}')
         all_rows = group * rows
         query_at = me * rows + lax.rem(lax.broadcasted_iota(jnp.int32, (hpg * rows, KEY_BLOCK), 0), rows)
         key_at = lax.broadcasted_iota(jnp.int32, (hpg * rows, KEY_BLOCK), 1)
         per_block = KEY_BLOCK // rows
+        stores = ((scores_a, max_a), (scores_b, max_b))
+        for g in range(CORES):
+            lanes = slice(g * half, (g + 1) * half)
+            score(stack_heads(queries[:, lanes], head_dim, scale),
+                  lambda start: k_all[start // rows:start // rows + per_block, :, lanes].reshape(KEY_BLOCK, half),
+                  all_rows, lambda start: key_at + start <= query_at, *stores[g])
         attended = []
         for g in range(CORES):
             lanes = slice(g * half, (g + 1) * half)
-            num, _, den = attend(
-                stack_heads(queries[:, lanes], head_dim, scale),
-                lambda start: k_all[start // rows:start // rows + per_block, :, lanes].reshape(KEY_BLOCK, half),
-                lambda start: v_all[start // rows:start // rows + per_block, :, lanes].reshape(KEY_BLOCK, half),
-                all_rows, lambda start: key_at + start <= query_at, scores_ref)
+            num, _, den = gather_values(
+                lambda start: v_all[start // rows:start // rows + per_block, :, lanes].reshape(KEY_BLOCK, half), all_rows, *stores[g])
             attended.append(unstack_heads(num / den, rows, head_dim).astype(BF16))
         attended = jnp.concatenate(attended, axis=-1)
+        phase(f'oproj{layer}')
         weight_copy('self_o', layer).wait()
         hidden = (hid[...].astype(F32) + mm(attended, w['self_o'][layer])).astype(BF16)
         hid[...] = hidden
 
+        phase(f'qproj{layer}')
         weight_copy('cross_q', layer).wait()
         queries = mm(rms_norm(hidden, norm_cross[layer:layer + 1, :]), w['cross_q'][layer]).astype(BF16)
         for g in range(CORES):
             q_send[layer, g] = queries[:, g * half:(g + 1) * half]
-        q_to_partner(layer).start()
-        for d in (1, 3, 2):
-            if d < chips:
-                for k in range(CORES):
-                    q_copy(layer, d, k).start()
+        q_order = [(d, k) for t in range(1, chips) for k, d in ((0, chips - t), (1, t))]
+
+        @pl.when(chip < mem_chips)
+        def _():
+            q_to_partner(layer).start()
+        for d, k in q_order:
+            @pl.when(lax.rem(chip + d, chips) < mem_chips)
+            def _():
+                q_copy(layer, d, k).start()
         q_all[layer, me] = q_send[layer, core]
 
         mem_at = chip * (CORES * mem_rows) + lax.broadcasted_iota(jnp.int32, (1, KEY_BLOCK), 1)
-        last = group - 1
-
-        def chunk(j, carry):
-            is_last = j // last
-            is_first = 1 - (j + last - 1) // last
-            mid = 1 - is_first - is_last
-            pair = (j + 1) // CORES - 1
-            d = mid * (1 + CORES * pair - 3 * (pair // 2))
-            k = is_first * core + is_last * (1 - core) + mid * lax.rem(j + 1, CORES)
-            src = lax.rem(chip + d, chips) * CORES + k
-
-            @pl.when(j > 0)
-            def _():
-                q_arrival(layer, src).wait_recv()
-
-            num, top, den = attend(
-                stack_heads(q_all[layer, src], head_dim, scale),
-                lambda start: mem_k[layer, start:start + KEY_BLOCK, :],
-                lambda start: mem_vals[layer, start:start + KEY_BLOCK, :],
-                CORES * mem_rows, lambda start: mem_at + start < mem_len_ref[0], scores_ref)
+        n_keys = CORES * mem_rows
+
+        def source(turn, second):
+            low = 1 - (turn + chips - 1) // chips
+            d = turn * (1 - core) + (chips - turn) * core
+            k = low * (core + second - 2 * core * second) + (1 - low) * second
+            return lax.rem(chip + d, chips) * CORES + k
+
+        def score_of(src, scores_ref, max_ref):
+            score(stack_heads(q_all[layer, src], head_dim, scale), lambda start: mem_k[layer, start:start + KEY_BLOCK, :], n_keys,
+                  lambda start: mem_at + start < mem_len_ref[0], scores_ref, max_ref)
+
+        def values_of(scores_ref, max_ref):
+            num, top, den = gather_values(lambda start: mem_vals[layer, start:start + KEY_BLOCK, :], n_keys, scores_ref, max_ref)
             part = unstack_heads(num, rows, head_dim).astype(BF16)
             lane = lax.broadcasted_iota(jnp.int32, (rows, 128), 1)
             stats = jnp.zeros((rows, 128), F32)
             for h in range(hpg):
                 stats = jnp.where(lane == h, top[h * rows:(h + 1) * rows], stats)
                 stats = jnp.where(lane == hpg + h, den[h * rows:(h + 1) * rows], stats)
-            stats = jnp.transpose(stats)[:2 * hpg]
-
-            @pl.when(j == 0)
-            def _():
-                part_recv[layer, me] = part
-                stat_recv[layer, me] = stats
-
-            @pl.when(j > 0)
-            def _():
-                part_send[layer, src] = part
-                stat_send[layer, src] = stats
-                part_copy(layer, src).start()
-                stat_copy(layer, src).start()
+            return part, jnp.transpose(stats)[:2 * hpg]
+
+        def put(src, part, stats):
+            part_send[layer, src] = part
+            stat_send[layer, src] = stats
+
+        def send(src):
+            part_copy(layer, src).start()
+            stat_copy(layer, src).start()
+
+        phase(f'cross{layer}')
+
+        def turn_body(turn, carry):
+            first, second = source(turn, 0), source(turn, 1)
+            q_arrival(layer, second).wait_recv()
+            score_of(second, scores_b, max_b)
+            put(first, *values_of(scores_a, max_a))
+
+            @pl.when(turn > 0)
+            def _():
+                send(first)
+            after = source(lax.rem(turn + 1, chips), 0)
+
+            @pl.when(turn < chips - 1)
+            def _():
+                q_arrival(layer, after).wait_recv()
+            score_of(after, scores_a, max_a)
+            put(second, *values_of(scores_b, max_b))
+            send(second)
             return carry
 
-        lax.fori_loop(0, group, chunk, 0)
-
-        def arrived(step, carry):
-            src = lax.rem(me + step, group)
-            stat_arrival(layer, src).wait_recv()
-            part_arrival(layer, src).wait_recv()
-            return carry
-
-        lax.fori_loop(1, group, arrived, 0)
-
-        factors = [None] * group
+        @pl.when(chip < mem_chips)
+        def _():
+            score_of(me, scores_a, max_a)
+            lax.fori_loop(0, chips, turn_body, 0)
+            part_recv[layer, me] = part_send[layer, me]
+            stat_recv[layer, me] = stat_send[layer, me]
+        phase(f'arrived{layer}')
+
+        for src in range(mem_chips * CORES):
+            @pl.when(src != me)
+            def _():
+                stat_arrival(layer, src).wait_recv()
+                part_arrival(layer, src).wait_recv()
+
+        phase(f'combine{layer}')
+        factors = [None] * (mem_chips * CORES)
         for g in range(CORES):
-            members = [c * CORES + g for c in range(chips)]
+            members = [c * CORES + g for c in range(mem_chips)]
             tops = [stat_recv[layer, i, 0:hpg] for i in members]
             dens = [stat_recv[layer, i, hpg:2 * hpg] for i in members]
             best = functools.reduce(jnp.maximum, tops)
@@ -329,13 +385,13 @@
             total = functools.reduce(jnp.add, [s * d for s, d in zip(shares, dens)])
             for i, s in zip(members, shares):
                 factors[i] = s / total
-        packed = jnp.concatenate(factors + [jnp.zeros((128 - group * hpg, rows), F32)], axis=0)
+        packed = jnp.concatenate(factors + [jnp.zeros((128 - mem_chips * CORES * hpg, rows), F32)], axis=0)
         packed = jnp.transpose(packed)
         lane_group = lane_groups(rows, half, head_dim)
         attended = []
         for g in range(CORES):
             total = jnp.zeros((rows, half), F32)
-            for c in range(chips):
+            for c in range(mem_chips):
                 i = c * CORES + g
                 factor = jnp.zeros((rows, half), F32)
                 for h in range(hpg):
@@ -343,9 +399,11 @@
                 total = total + part_recv[layer, i].astype(F32) * factor
             attended.append(total.astype(BF16))
         attended = jnp.concatenate(attended, axis=-1)
+        phase(f'co{layer}')
         weight_copy('cross_o', layer).wait()
         hidden = (hid[...].astype(F32) + mm(attended, w['cross_o'][layer])).astype(BF16)
 
+        phase(f'mlp{layer}')
         normed = rms_norm(hidden, norm_mlp[layer:layer + 1, :])
         for name in ('mlp_gate', 'mlp_up', 'mlp_down'):
             weight_copy(name, layer).wait()
@@ -360,9 +418,12 @@
         hidden = (hidden.astype(F32) + update).astype(BF16)
         hid[...] = hidden
 
+    phase('end')
     out_ref[...] = hid[...]
 
-    mem_out.wait_send()
+    @pl.when(chip < mem_chips)
+    def _():
+        mem_out.wait_send()
     for layer in range(n_layers):
         for d in range(1, chips):
             @pl.when(chip + d < chips)
@@ -373,21 +434,22 @@
             def _():
                 x_relayed(layer, d).wait_send()
 
-            for k in range(CORES):
-                q_copy(layer, d, k).wait_send()
+            @pl.when(lax.rem(chip + d, chips) < mem_chips)
+            def _():
+                for k in range(CORES):
+                    q_copy(layer, d, k).wait_send()
 
         @pl.when(core == 0)
         def _():
             x_to_partner(layer).wait_send()
-        q_to_partner(layer).wait_send()
-
-        def sent(step, carry):
-            src = lax.rem(me + step, group)
-            part_copy(layer, src).wait_send()
-            stat_copy(layer, src).wait_send()
-            return carry
-
-        lax.fori_loop(1, group, sent, 0)
+
+        @pl.when(chip < mem_chips)
+        def _():
+            q_to_partner(layer).wait_send()
+            for step in range(1, group):
+                part_copy(layer, lax.rem(me + step, group)).wait_send()
+                stat_copy(layer, lax.rem(me + step, group)).wait_send()
+    phase(None)
 
 
 def solution(mesh):
@@ -430,6 +492,9 @@
                 pltpu.VMEM((n_layers, group, 2 * hpg, rows), F32),
                 pltpu.VMEM((rows, width), BF16),
                 pltpu.VMEM((hpg * rows, all_keys), F32),
+                pltpu.VMEM((hpg * rows, all_keys), F32),
+                pltpu.VMEM((hpg * rows, 128), F32),
+                pltpu.VMEM((hpg * rows, 128), F32),
                 dma((len(WEIGHTS), n_layers)),
                 dma((1,)), dma((1,)), dma((1,)),
                 dma((n_layers, group // CORES)), dma((n_layers, group // CORES)), dma((n_layers, group)),

time: 93.8 us -> 80.8 us (0.86)
  the two profiles are of different devices: /device:TPU:112 before, /device:TPU:115 now
where the time goes in v2:
time: 80.8 us; the launch traced here: 80.7 us
  Pallas kernels  78.4 us (97%)
  local copies, waits for them, and re-layouts  1.57 us (2%)
    pallas_call x1, Pallas kernels, local_step(): pl.pallas_call(functools.partial(kernel, group, n_layers, head_dim), out_...  78.4 us

profile of v2, /device:TPU:115, one launch (start us, length us, event | category | flops | bytes accessed | tf_op | source)
XLA Modules:
  0.0 80.7 jit_solution(8086934435419922354)
XLA Ops:
  0.7 78.4 %shard_map.163 = bf16[128,512]{1,0:T(8,128)(2,1)} custom-call(bf16[128,512]{1,0:T(8,128)(2,1)} %refs_0_.1, bf16[1024,512]{1,0:T(8,128)(2,1)} %refs_1_.1, s32[1]{0:T(128)S(6)} %copy.19.refs_2_, bf16[2,512]{1,0:T(2,128)(2,1)} %refs_3_.1, bf16[2,512]{1,0:T(2,128)(2,1)} %refs_4_.1, bf16[2,512]{1,0:T(2,128)(2,1)} %refs_5_.1, bf16[2,512,512]{2,1,0:T(8,128)(2,1)} %refs_6_.1, ...), custom_call_target="tpu_custom_call" | custom-call | tf_op jit(solution)/shard_map/pallas_call | solution.py:475
  79.1 1.6 %copy.20 = bf16[128,512]{1,0:T(8,128)(2,1)} copy(bf16[128,512]{1,0:T(8,128)(2,1)} %shard_map.163) | data formatting | bytes 262144

commit v3 on v2

--- a/solution.py
+++ b/solution.py
@@ -13,6 +13,7 @@
 KEY_BLOCK = 512
 FF_BLOCK = 512
 MEM_BLOCK = 256
+ROW_BLOCK = 64
 MEM_LEN_MAX = 6144
 F32 = jnp.float32
 BF16 = jnp.bfloat16
@@ -46,30 +47,39 @@
     return jnp.concatenate([jnp.where(group == h, scaled, 0.0).astype(BF16) for h in range(lanes // head_dim)], axis=0)
 
 
-def score(q_stack, key_block, n_keys, allowed, scores_ref, max_ref):
-    run_max = None
-    for start in range(0, n_keys, KEY_BLOCK):
+def score_steps(q_stack, key_block, n_keys, allowed, scores_ref):
+    def step(start):
         scores = mm_t(q_stack, key_block(start))
-        scores = jnp.where(allowed(start), scores, NEG_BIG)
-        scores_ref[:, start:start + KEY_BLOCK] = scores
-        for lane in range(0, KEY_BLOCK, 128):
-            tile = scores[:, lane:lane + 128]
-            run_max = tile if run_max is None else jnp.maximum(run_max, tile)
-    max_ref[...] = run_max
-
-
-def gather_values(value_block, n_keys, scores_ref, max_ref):
-    top = jnp.max(max_ref[...], axis=-1, keepdims=True)
-    run_sum = None
-    numerator = None
-    for start in range(0, n_keys, KEY_BLOCK):
-        weights = jnp.exp(scores_ref[:, start:start + KEY_BLOCK] - top)
-        for lane in range(0, KEY_BLOCK, 128):
-            tile = weights[:, lane:lane + 128]
-            run_sum = tile if run_sum is None else run_sum + tile
-        part = mm(weights.astype(BF16), value_block(start))
-        numerator = part if numerator is None else numerator + part
-    return numerator, top, jnp.sum(run_sum, axis=-1, keepdims=True)
+        scores_ref[:, start:start + KEY_BLOCK] = jnp.where(allowed(start), scores, NEG_BIG)
+    return [functools.partial(step, start) for start in range(0, n_keys, KEY_BLOCK)]
+
+
+def exponent_steps(n_keys, scores_ref, weights_ref, tops, dens):
+    def step(row):
+        at = slice(row, row + ROW_BLOCK)
+        top = jnp.max(functools.reduce(jnp.maximum, [scores_ref[at, lane:lane + 128] for lane in range(0, n_keys, 128)]), axis=-1, keepdims=True)
+        run_sum = None
+        for lane in range(0, n_keys, 256):
+            weights = jnp.exp(scores_ref[at, lane:lane + 256] - top)
+            weights_ref[at, lane:lane + 256] = weights.astype(BF16)
+            pair = weights[:, :128] + weights[:, 128:]
+            run_sum = pair if run_sum is None else run_sum + pair
+        tops.append(top)
+        dens.append(jnp.sum(run_sum, axis=-1, keepdims=True))
+    return [functools.partial(step, row) for row in range(0, scores_ref.shape[0], ROW_BLOCK)]
+
+
+def value_steps(value_block, n_keys, weights_ref, parts):
+    def step(start):
+        part = mm(weights_ref[:, start:start + KEY_BLOCK], value_block(start))
+        parts[:] = [part if not parts else parts[0] + part]
+    return [functools.partial(step, start) for start in range(0, n_keys, KEY_BLOCK)]
+
+
+def interleave(*lists):
+    order = sorted(((i + 0.5) / len(steps), n, i) for n, steps in enumerate(lists) for i in range(len(steps)))
+    for _, n, i in order:
+        lists[n][i]()
 
 
 def unstack_heads(stacked, rows, head_dim):
@@ -100,7 +110,7 @@
     out_ref = refs[6 + n_w]
     scratch = refs[7 + n_w:]
     w = dict(zip(WEIGHTS, scratch[:n_w]))
-    (mem_v, x_all, k_all, v_all, mem_k, mem_vals, q_send, q_all, part_send, part_recv, stat_send, stat_recv, hid, scores_a, scores_b, max_a, max_b,
+    (mem_v, x_all, k_all, v_all, mem_k, mem_vals, q_send, q_all, part_send, part_recv, stat_send, stat_recv, hid, scores_a, scores_b, weights_a, weights_b,
      w_sem, mem_sem, mem_send, mem_recv, x_send, x_relay, x_recv, q_ssem, q_rsem, p_ssem, p_rsem, s_ssem, s_rsem) = scratch[n_w:]
 
     rows, width = hidden_ref.shape
@@ -274,18 +284,26 @@
         query_at = me * rows + lax.rem(lax.broadcasted_iota(jnp.int32, (hpg * rows, KEY_BLOCK), 0), rows)
         key_at = lax.broadcasted_iota(jnp.int32, (hpg * rows, KEY_BLOCK), 1)
         per_block = KEY_BLOCK // rows
-        stores = ((scores_a, max_a), (scores_b, max_b))
-        for g in range(CORES):
+        stores = ((scores_a, weights_a), (scores_b, weights_b))
+        tops, dens, parts = [[], []], [[], []], [[], []]
+
+        def self_steps(g):
             lanes = slice(g * half, (g + 1) * half)
-            score(stack_heads(queries[:, lanes], head_dim, scale),
-                  lambda start: k_all[start // rows:start // rows + per_block, :, lanes].reshape(KEY_BLOCK, half),
-                  all_rows, lambda start: key_at + start <= query_at, *stores[g])
-        attended = []
-        for g in range(CORES):
-            lanes = slice(g * half, (g + 1) * half)
-            num, _, den = gather_values(
-                lambda start: v_all[start // rows:start // rows + per_block, :, lanes].reshape(KEY_BLOCK, half), all_rows, *stores[g])
-            attended.append(unstack_heads(num / den, rows, head_dim).astype(BF16))
+            s_ref, w_ref = stores[g]
+            return (
+                score_steps(stack_heads(queries[:, lanes], head_dim, scale),
+                            lambda start: k_all[start // rows:start // rows + per_block, :, lanes].reshape(KEY_BLOCK, half),
+                            all_rows, lambda start: key_at + start <= query_at, s_ref),
+                exponent_steps(all_rows, s_ref, w_ref, tops[g], dens[g]),
+                value_steps(lambda start: v_all[start // rows:start // rows + per_block, :, lanes].reshape(KEY_BLOCK, half),
+                            all_rows, w_ref, parts[g]))
+
+        steps = [self_steps(g) for g in range(CORES)]
+        interleave(steps[0][0])
+        interleave(steps[0][1], steps[1][0])
+        interleave(steps[0][2], steps[1][1])
+        interleave(steps[1][2])
+        attended = [unstack_heads(parts[g][0] / jnp.concatenate(dens[g], axis=0), rows, head_dim).astype(BF16) for g in range(CORES)]
         attended = jnp.concatenate(attended, axis=-1)
         phase(f'oproj{layer}')
         weight_copy('self_o', layer).wait()
@@ -297,7 +315,7 @@
         queries = mm(rms_norm(hidden, norm_cross[layer:layer + 1, :]), w['cross_q'][layer]).astype(BF16)
         for g in range(CORES):
             q_send[layer, g] = queries[:, g * half:(g + 1) * half]
-        q_order = [(d, k) for t in range(1, chips) for k, d in ((0, chips - t), (1, t))]
+        q_order = [(d, k) for d in (1, 3, 2) if d < chips for k in range(CORES)]
 
         @pl.when(chip < mem_chips)
         def _():
@@ -311,59 +329,71 @@
         mem_at = chip * (CORES * mem_rows) + lax.broadcasted_iota(jnp.int32, (1, KEY_BLOCK), 1)
         n_keys = CORES * mem_rows
 
-        def source(turn, second):
-            low = 1 - (turn + chips - 1) // chips
-            d = turn * (1 - core) + (chips - turn) * core
-            k = low * (core + second - 2 * core * second) + (1 - low) * second
-            return lax.rem(chip + d, chips) * CORES + k
-
-        def score_of(src, scores_ref, max_ref):
-            score(stack_heads(q_all[layer, src], head_dim, scale), lambda start: mem_k[layer, start:start + KEY_BLOCK, :], n_keys,
-                  lambda start: mem_at + start < mem_len_ref[0], scores_ref, max_ref)
-
-        def values_of(scores_ref, max_ref):
-            num, top, den = gather_values(lambda start: mem_vals[layer, start:start + KEY_BLOCK, :], n_keys, scores_ref, max_ref)
-            part = unstack_heads(num, rows, head_dim).astype(BF16)
+        def wait_queries(src):
+            @pl.when(src != me)
+            def _():
+                q_arrival(layer, src).wait_recv()
+
+        def score_of(src, scores_ref):
+            return score_steps(stack_heads(q_all[layer, src], head_dim, scale), lambda start: mem_k[layer, start:start + KEY_BLOCK, :], n_keys,
+                               lambda start: mem_at + start < mem_len_ref[0], scores_ref)
+
+        def put_stats(src, tops, dens):
+            top, den = jnp.concatenate(tops, axis=0), jnp.concatenate(dens, axis=0)
             lane = lax.broadcasted_iota(jnp.int32, (rows, 128), 1)
             stats = jnp.zeros((rows, 128), F32)
             for h in range(hpg):
                 stats = jnp.where(lane == h, top[h * rows:(h + 1) * rows], stats)
                 stats = jnp.where(lane == hpg + h, den[h * rows:(h + 1) * rows], stats)
-            return part, jnp.transpose(stats)[:2 * hpg]
-
-        def put(src, part, stats):
-            part_send[layer, src] = part
-            stat_send[layer, src] = stats
-
-        def send(src):
-            part_copy(layer, src).start()
-            stat_copy(layer, src).start()
+            stat_send[layer, src] = jnp.transpose(stats)[:2 * hpg]
+
+        def values_of(weights_ref, parts):
+            return value_steps(lambda start: mem_vals[layer, start:start + KEY_BLOCK, :], n_keys, weights_ref, parts)
+
+        def put_part(src, parts):
+            part_send[layer, src] = unstack_heads(parts[0], rows, head_dim).astype(BF16)
+
+        def stages(after, s_after, now, s_now, w_now, before, w_before):
+            tops, dens, parts = [], [], []
+            interleave(score_of(after, s_after), exponent_steps(n_keys, s_now, w_now, tops, dens), values_of(w_before, parts))
+            put_stats(now, tops, dens)
+            put_part(before, parts)
+
+        def send(src, copy):
+            @pl.when(src != me)
+            def _():
+                copy(layer, src).start()
 
         phase(f'cross{layer}')
 
         def turn_body(turn, carry):
-            first, second = source(turn, 0), source(turn, 1)
-            q_arrival(layer, second).wait_recv()
-            score_of(second, scores_b, max_b)
-            put(first, *values_of(scores_a, max_a))
+            first = turn * 2
+            second, before, after = first + 1, lax.rem(first + group - 1, group), jnp.minimum(first + 2, group - 1)
+            wait_queries(second)
+            stages(second, scores_b, first, scores_a, weights_a, before, weights_b)
+            send(first, stat_copy)
 
             @pl.when(turn > 0)
             def _():
-                send(first)
-            after = source(lax.rem(turn + 1, chips), 0)
-
-            @pl.when(turn < chips - 1)
-            def _():
-                q_arrival(layer, after).wait_recv()
-            score_of(after, scores_a, max_a)
-            put(second, *values_of(scores_b, max_b))
-            send(second)
+                send(before, part_copy)
+
+            @pl.when(turn < group // 2 - 1)
+            def _():
+                wait_queries(first + 2)
+            stages(after, scores_a, second, scores_b, weights_b, first, weights_a)
+            send(second, stat_copy)
+            send(first, part_copy)
             return carry
 
         @pl.when(chip < mem_chips)
         def _():
-            score_of(me, scores_a, max_a)
-            lax.fori_loop(0, chips, turn_body, 0)
+            wait_queries(0)
+            interleave(score_of(0, scores_a))
+            lax.fori_loop(0, group // 2, turn_body, 0)
+            parts = []
+            interleave(values_of(weights_b, parts))
+            put_part(group - 1, parts)
+            send(group - 1, part_copy)
             part_recv[layer, me] = part_send[layer, me]
             stat_recv[layer, me] = stat_send[layer, me]
         phase(f'arrived{layer}')
@@ -493,8 +523,8 @@
                 pltpu.VMEM((rows, width), BF16),
                 pltpu.VMEM((hpg * rows, all_keys), F32),
                 pltpu.VMEM((hpg * rows, all_keys), F32),
-                pltpu.VMEM((hpg * rows, 128), F32),
-                pltpu.VMEM((hpg * rows, 128), F32),
+                pltpu.VMEM((hpg * rows, all_keys), BF16),
+                pltpu.VMEM((hpg * rows, all_keys), BF16),
                 dma((len(WEIGHTS), n_layers)),
                 dma((1,)), dma((1,)), dma((1,)),
                 dma((n_layers, group // CORES)), dma((n_layers, group // CORES)), dma((n_layers, group)),

time: 80.8 us -> 79.8 us (0.988)
  the two profiles are of different devices: /device:TPU:115 before, /device:TPU:127 now
where the time goes in v3:
time: 79.8 us; the launch traced here: 79.7 us
  Pallas kernels  77.4 us (97%)
  local copies, waits for them, and re-layouts  1.57 us (2%)
    pallas_call x1, Pallas kernels, local_step(): pl.pallas_call(functools.partial(kernel, group, n_layers, head_dim), out_...  77.4 us

profile of v3, /device:TPU:127, one launch (start us, length us, event | category | flops | bytes accessed | tf_op | source)
XLA Modules:
  0.0 79.7 jit_solution(580899603335144274)
XLA Ops:
  0.7 77.4 %shard_map.163 = bf16[128,512]{1,0:T(8,128)(2,1)} custom-call(bf16[128,512]{1,0:T(8,128)(2,1)} %refs_0_.1, bf16[1024,512]{1,0:T(8,128)(2,1)} %refs_1_.1, s32[1]{0:T(128)S(6)} %copy.19.refs_2_, bf16[2,512]{1,0:T(2,128)(2,1)} %refs_3_.1, bf16[2,512]{1,0:T(2,128)(2,1)} %refs_4_.1, bf16[2,512]{1,0:T(2,128)(2,1)} %refs_5_.1, bf16[2,512,512]{2,1,0:T(8,128)(2,1)} %refs_6_.1, ...), custom_call_target="tpu_custom_call" | custom-call | tf_op jit(solution)/shard_map/pallas_call | solution.py:505
  78.1 1.6 %copy.20 = bf16[128,512]{1,0:T(8,128)(2,1)} copy(bf16[128,512]{1,0:T(8,128)(2,1)} %shard_map.163) | data formatting | bytes 262144

commit v4 on v3

--- a/solution.py
+++ b/solution.py
@@ -14,6 +14,8 @@
 FF_BLOCK = 512
 MEM_BLOCK = 256
 ROW_BLOCK = 64
+LAG = 1
+LOWEST = -3.4e38
 MEM_LEN_MAX = 6144
 F32 = jnp.float32
 BF16 = jnp.bfloat16
@@ -54,16 +56,22 @@
     return [functools.partial(step, start) for start in range(0, n_keys, KEY_BLOCK)]
 
 
-def exponent_steps(n_keys, scores_ref, weights_ref, tops, dens):
+def exponent_steps(n_keys, scores_ref, weights_ref, tops, dens, lag=0):
+    sums = []
+
     def step(row):
         at = slice(row, row + ROW_BLOCK)
-        top = jnp.max(functools.reduce(jnp.maximum, [scores_ref[at, lane:lane + 128] for lane in range(0, n_keys, 128)]), axis=-1, keepdims=True)
+        tiles = [scores_ref[at, lane:lane + 128] for lane in range(0, n_keys, 128)]
+        if lag and len(sums) >= lag:
+            tiles.insert(0, jnp.minimum(sums[-lag], LOWEST))
+        top = jnp.max(functools.reduce(jnp.maximum, tiles), axis=-1, keepdims=True)
         run_sum = None
         for lane in range(0, n_keys, 256):
             weights = jnp.exp(scores_ref[at, lane:lane + 256] - top)
             weights_ref[at, lane:lane + 256] = weights.astype(BF16)
             pair = weights[:, :128] + weights[:, 128:]
             run_sum = pair if run_sum is None else run_sum + pair
+        sums.append(run_sum)
         tops.append(top)
         dens.append(jnp.sum(run_sum, axis=-1, keepdims=True))
     return [functools.partial(step, row) for row in range(0, scores_ref.shape[0], ROW_BLOCK)]
@@ -155,18 +163,42 @@
         pl.semaphore_signal(barrier, inc=1, device_id={'sp': lax.rem(me + step, group)}, device_id_type=MESH)
     pl.semaphore_wait(barrier, group - 1)
 
-    def x_to_chip(layer, d):
-        return remote(x_all.at[layer, me], x_all.at[layer, me], x_send.at[layer, d], x_recv.at[layer, me], me + d * CORES)
-
-    def x_to_partner(layer):
-        return remote(x_all.at[layer, me], x_all.at[layer, me], x_send.at[layer, 0], x_recv.at[layer, me], partner)
-
-    def x_relayed(layer, d):
-        src = me - d * CORES
-        return remote(x_all.at[layer, src], x_all.at[layer, src], x_relay.at[layer, d], x_recv.at[layer, src], partner)
-
-    def x_arrival(layer, src):
-        return remote(x_all.at[layer, src], x_all.at[layer, src], x_send.at[layer, 0], x_recv.at[layer, src], partner)
+    top_chip = chip // (chips - 1)
+    half_rows = rows // 2
+
+    def x_copy(layer, src, part, ssem, dst):
+        at = x_all.at[layer, src, pl.ds(pl.multiple_of(part * half_rows, half_rows), half_rows)]
+        return remote(at, at, ssem, x_recv.at[layer, src, part], dst)
+
+    def x_sends(layer):
+        up = me + CORES
+        across = (chips - 1) * CORES + core
+        send = x_send.at
+        return [
+            (chip == 1, x_copy(layer, me, 1, send[layer, 2], core)),
+            (chip < chips - 1, x_copy(layer, me, 0, send[layer, 0], up)),
+            (chip == 0, x_copy(layer, me, 1, send[layer, 2], across)),
+            (chip < chips - 1, x_copy(layer, me, 1, send[layer, 1], up)),
+            (chip == 0, x_copy(layer, me, 0, send[layer, 3], across)),
+            (core == 0, x_copy(layer, me, 0, send[layer, 4], partner)),
+            (core == 0, x_copy(layer, me, 1, send[layer, 5], partner)),
+        ]
+
+    def x_source(turn):
+        return top_chip * (turn * 2 - 3 * (turn // 2)) + (1 - top_chip) * (chip - 1 - turn)
+
+    def x_forward(layer):
+        src = x_source(0) * CORES + core
+        return x_copy(layer, src, top_chip, x_send.at[layer, 6], me + CORES - 2 * CORES * top_chip)
+
+    def x_forward_first(layer):
+        return x_copy(layer, CORES + core, 1, x_send.at[layer, 6], (chips - 1) * CORES + core)
+
+    def x_relay_copy(layer, turn, part):
+        return x_copy(layer, x_source(turn) * CORES + core, part, x_relay.at[layer, turn, part], partner)
+
+    def x_arrival(layer, src, part):
+        return x_copy(layer, src, part, x_send.at[layer, 0], partner)
 
     def q_copy(layer, d, k):
         dst = lax.rem(chip + d, chips) * CORES + k
@@ -193,14 +225,13 @@
     mem_out = remote(mem_v.at[core], mem_v.at[core], mem_send.at[0], mem_recv.at[0], partner)
     mem_in = remote(mem_v.at[1 - core], mem_v.at[1 - core], mem_send.at[0], mem_recv.at[0], partner)
 
-    def project_memory(slot):
+    def project_memory(slot, layer):
         def body(i, carry):
             at = pl.ds(pl.multiple_of(i * MEM_BLOCK, MEM_BLOCK), MEM_BLOCK)
             to = pl.ds(pl.multiple_of(slot * mem_rows + i * MEM_BLOCK, MEM_BLOCK), MEM_BLOCK)
             block = mem_v[slot, at, :]
-            for layer in range(n_layers):
-                mem_k[layer, to, :] = mm(block, w['cross_k'][layer]).astype(BF16)
-                mem_vals[layer, to, :] = mm(block, w['cross_v'][layer]).astype(BF16)
+            mem_k[layer, to, :] = mm(block, w['cross_k'][layer]).astype(BF16)
+            mem_vals[layer, to, :] = mm(block, w['cross_v'][layer]).astype(BF16)
             return carry
         lax.fori_loop(0, mem_rows // MEM_BLOCK, body, 0)
 
@@ -215,22 +246,11 @@
     for layer in range(n_layers):
         phase(f'xnorm{layer}')
         x_all[layer, me] = rms_norm(hid[...], norm_self[layer:layer + 1, :])
-        for d in (2, 1, 3):
-            if d < chips:
-                @pl.when(chip + d < chips)
-                def _():
-                    x_to_chip(layer, d).start()
-
-        @pl.when(core == 0)
-        def _():
-            x_to_partner(layer).start()
-
-        if layer == 0:
-            for name in ('self_q', 'self_k', 'self_v'):
-                weight_copy(name, layer).wait()
-        else:
-            for name in ('self_q', 'self_k', 'self_v'):
-                weight_copy(name, layer).wait()
+        for condition, copy in x_sends(layer):
+            pl.when(condition)(copy.start)
+
+        for name in ('self_q', 'self_k', 'self_v'):
+            weight_copy(name, layer).wait()
 
         def project_rows(src):
             block = x_all[layer, src]
@@ -251,33 +271,49 @@
             @pl.when(chip < mem_chips)
             def _():
                 mem_out.start()
-                project_memory(core)
+                for other in range(n_layers):
+                    project_memory(core, other)
         phase(f'xwait{layer}')
 
-        for d in range(1, chips):
-            @pl.when(chip - d >= 0)
-            def _():
-                x_arrival(layer, me - d * CORES).wait_recv()
-                x_relayed(layer, d).start()
-                project_rows(me - d * CORES)
-
+        @pl.when(chip == 0)
+        def _():
+            x_arrival(layer, CORES + core, 1).wait_recv()
+            x_forward_first(layer).start()
+
+        for turn in range(chips - 1):
+            @pl.when(turn < chip)
+            def _():
+                src = x_source(turn) * CORES + core
+                first = top_chip if turn == 0 else 0
+                for i, part in enumerate((first, 1 - first)):
+                    x_arrival(layer, src, part).wait_recv()
+                    if turn == 0 and i == 0:
+                        pl.when(chip > 0)(x_forward(layer).start)
+                    x_relay_copy(layer, turn, part).start()
+                project_rows(src)
+
+        phase(f'memproj2{layer}')
+
+        @pl.when(chip < mem_chips)
+        def _():
+            if layer == 0:
+                mem_in.wait_recv()
+            project_memory(1 - core, layer)
+
+        phase(f'xwait2{layer}')
         @pl.when(core == 1)
         def _():
-            x_arrival(layer, partner).wait_recv()
+            for part in (0, 1):
+                x_arrival(layer, partner, part).wait_recv()
             project_rows(partner)
 
-        for d in range(1, chips):
-            @pl.when(chip - d >= 0)
-            def _():
-                x_arrival(layer, partner - d * CORES).wait_recv()
-                project_rows(partner - d * CORES)
-
-        phase(f'memproj2{layer}')
-        if layer == 0:
-            @pl.when(chip < mem_chips)
-            def _():
-                mem_in.wait_recv()
-                project_memory(1 - core)
+        for turn in range(chips - 1):
+            @pl.when(turn < chip)
+            def _():
+                src = x_source(turn) * CORES + (1 - core)
+                for part in (0, 1):
+                    x_arrival(layer, src, part).wait_recv()
+                project_rows(src)
 
         phase(f'selfatt{layer}')
         all_rows = group * rows
@@ -355,7 +391,7 @@
 
         def stages(after, s_after, now, s_now, w_now, before, w_before):
             tops, dens, parts = [], [], []
-            interleave(score_of(after, s_after), exponent_steps(n_keys, s_now, w_now, tops, dens), values_of(w_before, parts))
+            interleave(score_of(after, s_after), exponent_steps(n_keys, s_now, w_now, tops, dens, LAG), values_of(w_before, parts))
             put_stats(now, tops, dens)
             put_part(before, parts)
 
@@ -455,23 +491,20 @@
     def _():
         mem_out.wait_send()
     for layer in range(n_layers):
+        for condition, copy in x_sends(layer):
+            pl.when(condition)(copy.wait_send)
+        pl.when(chip == 0)(x_forward_first(layer).wait_send)
+        pl.when(chip > 0)(x_forward(layer).wait_send)
+        for turn in range(chips - 1):
+            @pl.when(turn < chip)
+            def _():
+                for part in (0, 1):
+                    x_relay_copy(layer, turn, part).wait_send()
         for d in range(1, chips):
-            @pl.when(chip + d < chips)
-            def _():
-                x_to_chip(layer, d).wait_send()
-
-            @pl.when(chip - d >= 0)
-            def _():
-                x_relayed(layer, d).wait_send()
-
             @pl.when(lax.rem(chip + d, chips) < mem_chips)
             def _():
                 for k in range(CORES):
                     q_copy(layer, d, k).wait_send()
-
-        @pl.when(core == 0)
-        def _():
-            x_to_partner(layer).wait_send()
 
         @pl.when(chip < mem_chips)
         def _():
@@ -527,7 +560,7 @@
                 pltpu.VMEM((hpg * rows, all_keys), BF16),
                 dma((len(WEIGHTS), n_layers)),
                 dma((1,)), dma((1,)), dma((1,)),
-                dma((n_layers, group // CORES)), dma((n_layers, group // CORES)), dma((n_layers, group)),
+                dma((n_layers, 7)), dma((n_layers, group // CORES - 1, 2)), dma((n_layers, group, 2)),
                 dma((n_layers, group)), dma((n_layers, group)),
                 dma((n_layers, group)), dma((n_layers, group)),
                 dma((n_layers, group)), dma((n_layers, group)),

time: 79.8 us -> 77.1 us (0.966)
  Pallas kernels: 77.4 us -> 74.7 us
    pallas_call x1, Pallas kernels: 77.4 us -> 74.7 us  [local_step(): pl.pallas_call(functools.partial(kernel, group, n_layers, head_dim), out_...]
where the time goes in v4:
time: 77.1 us; the launch traced here: 77 us
  Pallas kernels  74.7 us (97%)
  local copies, waits for them, and re-layouts  1.57 us (2%)
    pallas_call x1, Pallas kernels, local_step(): pl.pallas_call(functools.partial(kernel, group, n_layers, head_dim), out_...  74.7 us
    unnamed x1, local copies, waits for them, and re-layouts  1.57 us

profile of v4, /device:TPU:127, one launch (start us, length us, event | category | flops | bytes accessed | tf_op | source)
XLA Modules:
  0.0 77.0 jit_solution(6801162350958290572)
XLA Ops:
  0.7 74.7 %shard_map.163 = bf16[128,512]{1,0:T(8,128)(2,1)} custom-call(bf16[128,512]{1,0:T(8,128)(2,1)} %refs_0_.1, bf16[1024,512]{1,0:T(8,128)(2,1)} %refs_1_.1, s32[1]{0:T(128)S(6)} %copy.19.refs_2_, bf16[2,512]{1,0:T(2,128)(2,1)} %refs_3_.1, bf16[2,512]{1,0:T(2,128)(2,1)} %refs_4_.1, bf16[2,512]{1,0:T(2,128)(2,1)} %refs_5_.1, bf16[2,512,512]{2,1,0:T(8,128)(2,1)} %refs_6_.1, ...), custom_call_target="tpu_custom_call" | custom-call | tf_op jit(solution)/shard_map/pallas_call | solution.py:538
  75.4 1.6 %copy.20 = bf16[128,512]{1,0:T(8,128)(2,1)} copy(bf16[128,512]{1,0:T(8,128)(2,1)} %shard_map.163) | data formatting | bytes 262144

commit v5 on v4

--- a/solution.py
+++ b/solution.py
@@ -151,10 +151,9 @@
     for layer in range(n_layers):
         for name in HALVED:
             weight_copy(name, layer).start()
-    for layer in range(n_layers):
-        for name in WEIGHTS:
-            if name in HALVED or (layer == 0 and name in ('self_q', 'self_k', 'self_v')):
-                continue
+
+    def start_weights(layer, names):
+        for name in names:
             weight_copy(name, layer).start()
 
     phase('barrier')
@@ -248,6 +247,8 @@
         x_all[layer, me] = rms_norm(hid[...], norm_self[layer:layer + 1, :])
         for condition, copy in x_sends(layer):
             pl.when(condition)(copy.start)
+        if layer == 0:
+            start_weights(0, ('self_o', 'cross_q', 'cross_o'))
 
         for name in ('self_q', 'self_k', 'self_v'):
             weight_copy(name, layer).wait()
@@ -361,6 +362,10 @@
             def _():
                 q_copy(layer, d, k).start()
         q_all[layer, me] = q_send[layer, core]
+        if layer == 0:
+            start_weights(0, ('mlp_gate', 'mlp_up', 'mlp_down'))
+            for other in range(1, n_layers):
+                start_weights(other, [name for name in WEIGHTS if name not in HALVED])
 
         mem_at = chip * (CORES * mem_rows) + lax.broadcasted_iota(jnp.int32, (1, KEY_BLOCK), 1)
         n_keys = CORES * mem_rows

time: 77.1 us -> 73.7 us (0.956)
  Pallas kernels: 74.7 us -> 71.3 us
    pallas_call x1, Pallas kernels: 74.7 us -> 71.3 us  [local_step(): pl.pallas_call(functools.partial(kernel, group, n_layers, head_dim), out_...]
where the time goes in v5:
time: 73.7 us; the launch traced here: 73.6 us
  Pallas kernels  71.3 us (97%)
  local copies, waits for them, and re-layouts  1.57 us (2%)
    pallas_call x1, Pallas kernels, local_step(): pl.pallas_call(functools.partial(kernel, group, n_layers, head_dim), out_...  71.3 us
    unnamed x1, local copies, waits for them, and re-layouts  1.57 us

profile of v5, /device:TPU:127, one launch (start us, length us, event | category | flops | bytes accessed | tf_op | source)
XLA Modules:
  0.0 73.6 jit_solution(2240396543733898921)
XLA Ops:
  0.7 71.3 %shard_map.163 = bf16[128,512]{1,0:T(8,128)(2,1)} custom-call(bf16[128,512]{1,0:T(8,128)(2,1)} %refs_0_.1, bf16[1024,512]{1,0:T(8,128)(2,1)} %refs_1_.1, s32[1]{0:T(128)S(6)} %copy.19.refs_2_, bf16[2,512]{1,0:T(2,128)(2,1)} %refs_3_.1, bf16[2,512]{1,0:T(2,128)(2,1)} %refs_4_.1, bf16[2,512]{1,0:T(2,128)(2,1)} %refs_5_.1, bf16[2,512,512]{2,1,0:T(8,128)(2,1)} %refs_6_.1, ...), custom_call_target="tpu_custom_call" | custom-call | tf_op jit(solution)/shard_map/pallas_call | solution.py:543
  72.0 1.6 %copy.20 = bf16[128,512]{1,0:T(8,128)(2,1)} copy(bf16[128,512]{1,0:T(8,128)(2,1)} %shard_map.163) | data formatting | bytes 262144

commit v6 on v5

--- a/solution.py
+++ b/solution.py
@@ -15,6 +15,7 @@
 MEM_BLOCK = 256
 ROW_BLOCK = 64
 LAG = 1
+X_ORDER = (2, 3, 1)
 LOWEST = -3.4e38
 MEM_LEN_MAX = 6144
 F32 = jnp.float32
@@ -170,34 +171,22 @@
         return remote(at, at, ssem, x_recv.at[layer, src, part], dst)
 
     def x_sends(layer):
-        up = me + CORES
-        across = (chips - 1) * CORES + core
-        send = x_send.at
-        return [
-            (chip == 1, x_copy(layer, me, 1, send[layer, 2], core)),
-            (chip < chips - 1, x_copy(layer, me, 0, send[layer, 0], up)),
-            (chip == 0, x_copy(layer, me, 1, send[layer, 2], across)),
-            (chip < chips - 1, x_copy(layer, me, 1, send[layer, 1], up)),
-            (chip == 0, x_copy(layer, me, 0, send[layer, 3], across)),
-            (core == 0, x_copy(layer, me, 0, send[layer, 4], partner)),
-            (core == 0, x_copy(layer, me, 1, send[layer, 5], partner)),
-        ]
+        sends = []
+        for d in X_ORDER:
+            for part in (0, 1):
+                sends.append((chip + d < chips, x_copy(layer, me, part, x_send.at[layer, d, part], me + d * CORES)))
+        for part in (0, 1):
+            sends.append((core == 0, x_copy(layer, me, part, x_send.at[layer, 0, part], partner)))
+        return sends
 
     def x_source(turn):
         return top_chip * (turn * 2 - 3 * (turn // 2)) + (1 - top_chip) * (chip - 1 - turn)
 
-    def x_forward(layer):
-        src = x_source(0) * CORES + core
-        return x_copy(layer, src, top_chip, x_send.at[layer, 6], me + CORES - 2 * CORES * top_chip)
-
-    def x_forward_first(layer):
-        return x_copy(layer, CORES + core, 1, x_send.at[layer, 6], (chips - 1) * CORES + core)
-
     def x_relay_copy(layer, turn, part):
         return x_copy(layer, x_source(turn) * CORES + core, part, x_relay.at[layer, turn, part], partner)
 
     def x_arrival(layer, src, part):
-        return x_copy(layer, src, part, x_send.at[layer, 0], partner)
+        return x_copy(layer, src, part, x_send.at[layer, 0, part], partner)
 
     def q_copy(layer, d, k):
         dst = lax.rem(chip + d, chips) * CORES + k
@@ -276,20 +265,12 @@
                     project_memory(core, other)
         phase(f'xwait{layer}')
 
-        @pl.when(chip == 0)
-        def _():
-            x_arrival(layer, CORES + core, 1).wait_recv()
-            x_forward_first(layer).start()
-
         for turn in range(chips - 1):
             @pl.when(turn < chip)
             def _():
                 src = x_source(turn) * CORES + core
-                first = top_chip if turn == 0 else 0
-                for i, part in enumerate((first, 1 - first)):
+                for part in (0, 1):
                     x_arrival(layer, src, part).wait_recv()
-                    if turn == 0 and i == 0:
-                        pl.when(chip > 0)(x_forward(layer).start)
                     x_relay_copy(layer, turn, part).start()
                 project_rows(src)
 
@@ -498,8 +479,6 @@
     for layer in range(n_layers):
         for condition, copy in x_sends(layer):
             pl.when(condition)(copy.wait_send)
-        pl.when(chip == 0)(x_forward_first(layer).wait_send)
-        pl.when(chip > 0)(x_forward(layer).wait_send)
         for turn in range(chips - 1):
             @pl.when(turn < chip)
             def _():
@@ -565,7 +544,7 @@
                 pltpu.VMEM((hpg * rows, all_keys), BF16),
                 dma((len(WEIGHTS), n_layers)),
                 dma((1,)), dma((1,)), dma((1,)),
-                dma((n_layers, 7)), dma((n_layers, group // CORES - 1, 2)), dma((n_layers, group, 2)),
+                dma((n_layers, group // CORES, 2)), dma((n_layers, group // CORES - 1, 2)), dma((n_layers, group, 2)),
                 dma((n_layers, group)), dma((n_layers, group)),
                 dma((n_layers, group)), dma((n_layers, group)),
                 dma((n_layers, group)), dma((n_layers, group)),

time: 73.7 us -> 75.4 us (1.023)
  Pallas kernels: 71.3 us -> 73 us
    pallas_call x1, Pallas kernels: 71.3 us -> 73 us  [local_step(): pl.pallas_call(functools.partial(kernel, group, n_layers, head_dim), out_...]
where the time goes in v6:
time: 75.4 us; the launch traced here: 75.3 us
  Pallas kernels  73 us (97%)
  local copies, waits for them, and re-layouts  1.57 us (2%)
    pallas_call x1, Pallas kernels, local_step(): pl.pallas_call(functools.partial(kernel, group, n_layers, head_dim), out_...  73 us
    unnamed x1, local copies, waits for them, and re-layouts  1.57 us

profile of v6, /device:TPU:127, one launch (start us, length us, event | category | flops | bytes accessed | tf_op | source)
XLA Modules:
  0.0 75.3 jit_solution(11780081140253142544)
XLA Ops:
  0.7 73.0 %shard_map.163 = bf16[128,512]{1,0:T(8,128)(2,1)} custom-call(bf16[128,512]{1,0:T(8,128)(2,1)} %refs_0_.1, bf16[1024,512]{1,0:T(8,128)(2,1)} %refs_1_.1, s32[1]{0:T(128)S(6)} %copy.19.refs_2_, bf16[2,512]{1,0:T(2,128)(2,1)} %refs_3_.1, bf16[2,512]{1,0:T(2,128)(2,1)} %refs_4_.1, bf16[2,512]{1,0:T(2,128)(2,1)} %refs_5_.1, bf16[2,512,512]{2,1,0:T(8,128)(2,1)} %refs_6_.1, ...), custom_call_target="tpu_custom_call" | custom-call | tf_op jit(solution)/shard_map/pallas_call | solution.py:522
  73.7 1.6 %copy.20 = bf16[128,512]{1,0:T(8,128)(2,1)} copy(bf16[128,512]{1,0:T(8,128)(2,1)} %shard_map.163) | data formatting | bytes 262144

commit v7 on v5

--- a/solution.py
+++ b/solution.py
@@ -174,13 +174,13 @@
         across = (chips - 1) * CORES + core
         send = x_send.at
         return [
+            (core == 0, x_copy(layer, me, 0, send[layer, 4], partner)),
+            (core == 0, x_copy(layer, me, 1, send[layer, 5], partner)),
             (chip == 1, x_copy(layer, me, 1, send[layer, 2], core)),
             (chip < chips - 1, x_copy(layer, me, 0, send[layer, 0], up)),
             (chip == 0, x_copy(layer, me, 1, send[layer, 2], across)),
             (chip < chips - 1, x_copy(layer, me, 1, send[layer, 1], up)),
             (chip == 0, x_copy(layer, me, 0, send[layer, 3], across)),
-            (core == 0, x_copy(layer, me, 0, send[layer, 4], partner)),
-            (core == 0, x_copy(layer, me, 1, send[layer, 5], partner)),
         ]
 
     def x_source(turn):
@@ -362,10 +362,10 @@
             def _():
                 q_copy(layer, d, k).start()
         q_all[layer, me] = q_send[layer, core]
+        later = []
         if layer == 0:
-            start_weights(0, ('mlp_gate', 'mlp_up', 'mlp_down'))
-            for other in range(1, n_layers):
-                start_weights(other, [name for name in WEIGHTS if name not in HALVED])
+            later = [(0, name) for name in ('mlp_gate', 'mlp_up', 'mlp_down')]
+            later += [(other, name) for other in range(1, n_layers) for name in WEIGHTS if name not in HALVED]
 
         mem_at = chip * (CORES * mem_rows) + lax.broadcasted_iota(jnp.int32, (1, KEY_BLOCK), 1)
         n_keys = CORES * mem_rows
@@ -409,6 +409,12 @@
 
         def turn_body(turn, carry):
             first = turn * 2
+            for i in range(group // 2):
+                if later:
+                    @pl.when(turn == i)
+                    def _():
+                        for other, name in later[i::group // 2]:
+                            weight_copy(name, other).start()
             second, before, after = first + 1, lax.rem(first + group - 1, group), jnp.minimum(first + 2, group - 1)
             wait_queries(second)
             stages(second, scores_b, first, scores_a, weights_a, before, weights_b)
@@ -437,6 +443,11 @@
             send(group - 1, part_copy)
             part_recv[layer, me] = part_send[layer, me]
             stat_recv[layer, me] = stat_send[layer, me]
+
+        @pl.when(chip >= mem_chips)
+        def _():
+            for other, name in later:
+                weight_copy(name, other).start()
         phase(f'arrived{layer}')
 
         for src in range(mem_chips * CORES):

time: 73.7 us -> 73.8 us (level)
  no operation moved by 1% of the time
where the time goes in v7:
time: 73.8 us; the launch traced here: 73.7 us
  Pallas kernels  71.4 us (97%)
  local copies, waits for them, and re-layouts  1.57 us (2%)
    pallas_call x1, Pallas kernels, local_step(): pl.pallas_call(functools.partial(kernel, group, n_layers, head_dim), out_...  71.4 us
    unnamed x1, local copies, waits for them, and re-layouts  1.57 us

profile of v7, /device:TPU:127, one launch (start us, length us, event | category | flops | bytes accessed | tf_op | source)
XLA Modules:
  0.0 73.7 jit_solution(7162022697132114155)
XLA Ops:
  0.7 71.4 %shard_map.163 = bf16[128,512]{1,0:T(8,128)(2,1)} custom-call(bf16[128,512]{1,0:T(8,128)(2,1)} %refs_0_.1, bf16[1024,512]{1,0:T(8,128)(2,1)} %refs_1_.1, s32[1]{0:T(128)S(6)} %copy.19.refs_2_, bf16[2,512]{1,0:T(2,128)(2,1)} %refs_3_.1, bf16[2,512]{1,0:T(2,128)(2,1)} %refs_4_.1, bf16[2,512]{1,0:T(2,128)(2,1)} %refs_5_.1, bf16[2,512,512]{2,1,0:T(8,128)(2,1)} %refs_6_.1, ...), custom_call_target="tpu_custom_call" | custom-call | tf_op jit(solution)/shard_map/pallas_call | solution.py:554
  72.1 1.6 %copy.20 = bf16[128,512]{1,0:T(8,128)(2,1)} copy(bf16[128,512]{1,0:T(8,128)(2,1)} %shard_map.163) | data formatting | bytes 262144

commit v8 on v7

--- a/solution.py
+++ b/solution.py
@@ -11,6 +11,7 @@
 NEG_BIG = -1e30
 CORES = 2
 KEY_BLOCK = 512
+VALUE_BLOCK = 2048
 FF_BLOCK = 512
 MEM_BLOCK = 256
 ROW_BLOCK = 64
@@ -79,9 +80,10 @@
 
 def value_steps(value_block, n_keys, weights_ref, parts):
     def step(start):
-        part = mm(weights_ref[:, start:start + KEY_BLOCK], value_block(start))
+        stop = min(start + VALUE_BLOCK, n_keys)
+        part = mm(weights_ref[:, start:stop], value_block(start, stop))
         parts[:] = [part if not parts else parts[0] + part]
-    return [functools.partial(step, start) for start in range(0, n_keys, KEY_BLOCK)]
+    return [functools.partial(step, start) for start in range(0, n_keys, VALUE_BLOCK)]
 
 
 def interleave(*lists):
@@ -332,7 +334,7 @@
                             lambda start: k_all[start // rows:start // rows + per_block, :, lanes].reshape(KEY_BLOCK, half),
                             all_rows, lambda start: key_at + start <= query_at, s_ref),
                 exponent_steps(all_rows, s_ref, w_ref, tops[g], dens[g]),
-                value_steps(lambda start: v_all[start // rows:start // rows + per_block, :, lanes].reshape(KEY_BLOCK, half),
+                value_steps(lambda start, stop: v_all[start // rows:stop // rows, :, lanes].reshape(stop - start, half),
                             all_rows, w_ref, parts[g]))
 
         steps = [self_steps(g) for g in range(CORES)]
@@ -389,7 +391,7 @@
             stat_send[layer, src] = jnp.transpose(stats)[:2 * hpg]
 
         def values_of(weights_ref, parts):
-            return value_steps(lambda start: mem_vals[layer, start:start + KEY_BLOCK, :], n_keys, weights_ref, parts)
+            return value_steps(lambda start, stop: mem_vals[layer, start:stop, :], n_keys, weights_ref, parts)
 
         def put_part(src, parts):
             part_send[layer, src] = unstack_heads(parts[0], rows, head_dim).astype(BF16)

time: 73.8 us -> 73.8 us (level)
  no operation moved by 1% of the time
where the time goes in v8:
time: 73.8 us; the launch traced here: 73.7 us
  Pallas kernels  71.5 us (97%)
  local copies, waits for them, and re-layouts  1.57 us (2%)
    pallas_call x1, Pallas kernels, local_step(): pl.pallas_call(functools.partial(kernel, group, n_layers, head_dim), out_...  71.5 us
    unnamed x1, local copies, waits for them, and re-layouts  1.57 us

profile of v8, /device:TPU:127, one launch (start us, length us, event | category | flops | bytes accessed | tf_op | source)
XLA Modules:
  0.0 73.7 jit_solution(7759612360743064823)
XLA Ops:
  0.7 71.5 %shard_map.163 = bf16[128,512]{1,0:T(8,128)(2,1)} custom-call(bf16[128,512]{1,0:T(8,128)(2,1)} %refs_0_.1, bf16[1024,512]{1,0:T(8,128)(2,1)} %refs_1_.1, s32[1]{0:T(128)S(6)} %copy.19.refs_2_, bf16[2,512]{1,0:T(2,128)(2,1)} %refs_3_.1, bf16[2,512]{1,0:T(2,128)(2,1)} %refs_4_.1, bf16[2,512]{1,0:T(2,128)(2,1)} %refs_5_.1, bf16[2,512,512]{2,1,0:T(8,128)(2,1)} %refs_6_.1, ...), custom_call_target="tpu_custom_call" | custom-call | tf_op jit(solution)/shard_map/pallas_call | solution.py:556
  72.2 1.6 %copy.20 = bf16[128,512]{1,0:T(8,128)(2,1)} copy(bf16[128,512]{1,0:T(8,128)(2,1)} %shard_map.163) | data formatting | bytes 262144

commit v9 on v8

--- a/solution.py
+++ b/solution.py
@@ -409,15 +409,20 @@
 
         phase(f'cross{layer}')
 
+        def pair(turn):
+            return turn + (chip // (mem_chips - 1)) * (turn // 2) * (1 - 2 * lax.rem(turn, 2))
+
         def turn_body(turn, carry):
-            first = turn * 2
+            first = pair(turn) * CORES
             for i in range(group // 2):
                 if later:
                     @pl.when(turn == i)
                     def _():
                         for other, name in later[i::group // 2]:
                             weight_copy(name, other).start()
-            second, before, after = first + 1, lax.rem(first + group - 1, group), jnp.minimum(first + 2, group - 1)
+            second = first + 1
+            before = pair(lax.rem(turn + chips - 1, chips)) * CORES + 1
+            after = pair(lax.rem(turn + 1, chips)) * CORES
             wait_queries(second)
             stages(second, scores_b, first, scores_a, weights_a, before, weights_b)
             send(first, stat_copy)
@@ -426,9 +431,9 @@
             def _():
                 send(before, part_copy)
 
-            @pl.when(turn < group // 2 - 1)
-            def _():
-                wait_queries(first + 2)
+            @pl.when(turn < chips - 1)
+            def _():
+                wait_queries(after)
             stages(after, scores_a, second, scores_b, weights_b, first, weights_a)
             send(second, stat_copy)
             send(first, part_copy)
@@ -438,11 +443,12 @@
         def _():
             wait_queries(0)
             interleave(score_of(0, scores_a))
-            lax.fori_loop(0, group // 2, turn_body, 0)
+            lax.fori_loop(0, chips, turn_body, 0)
             parts = []
             interleave(values_of(weights_b, parts))
-            put_part(group - 1, parts)
-            send(group - 1, part_copy)
+            last = pair(jnp.int32(chips - 1)) * CORES + 1
+            put_part(last, parts)
+            send(last, part_copy)
             part_recv[layer, me] = part_send[layer, me]
             stat_recv[layer, me] = stat_send[layer, me]
 

time: 73.8 us -> 74 us (level)
  no operation moved by 1% of the time
where the time goes in v9:
time: 74 us; the launch traced here: 73.9 us
  Pallas kernels  71.7 us (97%)
  local copies, waits for them, and re-layouts  1.57 us (2%)
    pallas_call x1, Pallas kernels, local_step(): pl.pallas_call(functools.partial(kernel, group, n_layers, head_dim), out_...  71.7 us
    unnamed x1, local copies, waits for them, and re-layouts  1.57 us

profile of v9, /device:TPU:127, one launch (start us, length us, event | category | flops | bytes accessed | tf_op | source)
XLA Modules:
  0.0 73.9 jit_solution(5974724819055442722)
XLA Ops:
  0.7 71.7 %shard_map.163 = bf16[128,512]{1,0:T(8,128)(2,1)} custom-call(bf16[128,512]{1,0:T(8,128)(2,1)} %refs_0_.1, bf16[1024,512]{1,0:T(8,128)(2,1)} %refs_1_.1, s32[1]{0:T(128)S(6)} %copy.19.refs_2_, bf16[2,512]{1,0:T(2,128)(2,1)} %refs_3_.1, bf16[2,512]{1,0:T(2,128)(2,1)} %refs_4_.1, bf16[2,512]{1,0:T(2,128)(2,1)} %refs_5_.1, bf16[2,512,512]{2,1,0:T(8,128)(2,1)} %refs_6_.1, ...), custom_call_target="tpu_custom_call" | custom-call | tf_op jit(solution)/shard_map/pallas_call | solution.py:562
  72.4 1.6 %copy.20 = bf16[128,512]{1,0:T(8,128)(2,1)} copy(bf16[128,512]{1,0:T(8,128)(2,1)} %shard_map.163) | data formatting | bytes 262144

commit v10 on v9

--- a/solution.py
+++ b/solution.py
@@ -188,9 +188,8 @@
     def x_source(turn):
         return top_chip * (turn * 2 - 3 * (turn // 2)) + (1 - top_chip) * (chip - 1 - turn)
 
-    def x_forward(layer):
-        src = x_source(0) * CORES + core
-        return x_copy(layer, src, top_chip, x_send.at[layer, 6], me + CORES - 2 * CORES * top_chip)
+    def x_forward(layer, part):
+        return x_copy(layer, x_source(0) * CORES + core, part, x_send.at[layer, 6 + part], me + CORES)
 
     def x_forward_first(layer):
         return x_copy(layer, CORES + core, 1, x_send.at[layer, 6], (chips - 1) * CORES + core)
@@ -276,32 +275,38 @@
                 mem_out.start()
                 for other in range(n_layers):
                     project_memory(core, other)
-        phase(f'xwait{layer}')
-
-        @pl.when(chip == 0)
-        def _():
-            x_arrival(layer, CORES + core, 1).wait_recv()
-            x_forward_first(layer).start()
-
-        for turn in range(chips - 1):
-            @pl.when(turn < chip)
-            def _():
-                src = x_source(turn) * CORES + core
-                first = top_chip if turn == 0 else 0
-                for i, part in enumerate((first, 1 - first)):
-                    x_arrival(layer, src, part).wait_recv()
-                    if turn == 0 and i == 0:
-                        pl.when(chip > 0)(x_forward(layer).start)
-                    x_relay_copy(layer, turn, part).start()
-                project_rows(src)
-
-        phase(f'memproj2{layer}')
-
-        @pl.when(chip < mem_chips)
-        def _():
+
+        def project_partner_memory():
             if layer == 0:
                 mem_in.wait_recv()
             project_memory(1 - core, layer)
+
+        @pl.when(chip == mem_chips - 1)
+        def _():
+            project_partner_memory()
+        phase(f'xwait{layer}')
+
+        @pl.when(chip == 0)
+        def _():
+            x_arrival(layer, CORES + core, 1).wait_recv()
+            x_forward_first(layer).start()
+
+        for turn in range(chips - 1):
+            @pl.when(turn < chip)
+            def _():
+                src = x_source(turn) * CORES + core
+                for part in (0, 1):
+                    x_arrival(layer, src, part).wait_recv()
+                    if turn == 0:
+                        pl.when(chip == 1 if part else chip < chips - 1)(x_forward(layer, part).start)
+                    x_relay_copy(layer, turn, part).start()
+                project_rows(src)
+
+        phase(f'memproj2{layer}')
+
+        @pl.when(chip < mem_chips - 1)
+        def _():
+            project_partner_memory()
 
         phase(f'xwait2{layer}')
         @pl.when(core == 1)
@@ -354,7 +359,7 @@
         queries = mm(rms_norm(hidden, norm_cross[layer:layer + 1, :]), w['cross_q'][layer]).astype(BF16)
         for g in range(CORES):
             q_send[layer, g] = queries[:, g * half:(g + 1) * half]
-        q_order = [(d, k) for d in (1, 3, 2) if d < chips for k in range(CORES)]
+        q_order = [(d, k) for d in (2, 1, 3) if d < chips for k in range(CORES)]
 
         @pl.when(chip < mem_chips)
         def _():
@@ -518,7 +523,8 @@
         for condition, copy in x_sends(layer):
             pl.when(condition)(copy.wait_send)
         pl.when(chip == 0)(x_forward_first(layer).wait_send)
-        pl.when(chip > 0)(x_forward(layer).wait_send)
+        for part in (0, 1):
+            pl.when((chip == 1) if part else (chip > 0) & (chip < chips - 1))(x_forward(layer, part).wait_send)
         for turn in range(chips - 1):
             @pl.when(turn < chip)
             def _():
@@ -584,7 +590,7 @@
                 pltpu.VMEM((hpg * rows, all_keys), BF16),
                 dma((len(WEIGHTS), n_layers)),
                 dma((1,)), dma((1,)), dma((1,)),
-                dma((n_layers, 7)), dma((n_layers, group // CORES - 1, 2)), dma((n_layers, group, 2)),
+                dma((n_layers, 8)), dma((n_layers, group // CORES - 1, 2)), dma((n_layers, group, 2)),
                 dma((n_layers, group)), dma((n_layers, group)),
                 dma((n_layers, group)), dma((n_layers, group)),
                 dma((n_layers, group)), dma((n_layers, group)),

time: 74 us -> 74.3 us (level)
  no operation moved by 1% of the time
where the time goes in v10:
time: 74.3 us; the launch traced here: 74.2 us
  Pallas kernels  72 us (97%)
  local copies, waits for them, and re-layouts  1.57 us (2%)
    pallas_call x1, Pallas kernels, local_step(): pl.pallas_call(functools.partial(kernel, group, n_layers, head_dim), out_...  72 us
    unnamed x1, local copies, waits for them, and re-layouts  1.57 us

profile of v10, /device:TPU:127, one launch (start us, length us, event | category | flops | bytes accessed | tf_op | source)
XLA Modules:
  0.0 74.2 jit_solution(1910364467937314385)
XLA Ops:
  0.7 72.0 %shard_map.163 = bf16[128,512]{1,0:T(8,128)(2,1)} custom-call(bf16[128,512]{1,0:T(8,128)(2,1)} %refs_0_.1, bf16[1024,512]{1,0:T(8,128)(2,1)} %refs_1_.1, s32[1]{0:T(128)S(6)} %copy.19.refs_2_, bf16[2,512]{1,0:T(2,128)(2,1)} %refs_3_.1, bf16[2,512]{1,0:T(2,128)(2,1)} %refs_4_.1, bf16[2,512]{1,0:T(2,128)(2,1)} %refs_5_.1, bf16[2,512,512]{2,1,0:T(8,128)(2,1)} %refs_6_.1, ...), custom_call_target="tpu_custom_call" | custom-call | tf_op jit(solution)/shard_map/pallas_call | solution.py:568
  72.6 1.6 %copy.20 = bf16[128,512]{1,0:T(8,128)(2,1)} copy(bf16[128,512]{1,0:T(8,128)(2,1)} %shard_map.163) | data formatting | bytes 262144

commit v11 on v10

--- a/solution.py
+++ b/solution.py
@@ -359,7 +359,7 @@
         queries = mm(rms_norm(hidden, norm_cross[layer:layer + 1, :]), w['cross_q'][layer]).astype(BF16)
         for g in range(CORES):
             q_send[layer, g] = queries[:, g * half:(g + 1) * half]
-        q_order = [(d, k) for d in (2, 1, 3) if d < chips for k in range(CORES)]
+        q_order = [(d, k) for d in (1, 3, 2) if d < chips for k in range(CORES)]
 
         @pl.when(chip < mem_chips)
         def _():

time: 74.3 us -> 71.9 us (0.968)
  Pallas kernels: 72 us -> 69.6 us
    pallas_call x1, Pallas kernels: 72 us -> 69.6 us  [local_step(): pl.pallas_call(functools.partial(kernel, group, n_layers, head_dim), out_...]
where the time goes in v11:
time: 71.9 us; the launch traced here: 71.8 us
  Pallas kernels  69.6 us (97%)
  local copies, waits for them, and re-layouts  1.57 us (2%)
    pallas_call x1, Pallas kernels, local_step(): pl.pallas_call(functools.partial(kernel, group, n_layers, head_dim), out_...  69.6 us
    unnamed x1, local copies, waits for them, and re-layouts  1.57 us

profile of v11, /device:TPU:127, one launch (start us, length us, event | category | flops | bytes accessed | tf_op | source)
XLA Modules:
  0.0 71.8 jit_solution(991515977387388293)
XLA Ops:
  0.7 69.6 %shard_map.163 = bf16[128,512]{1,0:T(8,128)(2,1)} custom-call(bf16[128,512]{1,0:T(8,128)(2,1)} %refs_0_.1, bf16[1024,512]{1,0:T(8,128)(2,1)} %refs_1_.1, s32[1]{0:T(128)S(6)} %copy.19.refs_2_, bf16[2,512]{1,0:T(2,128)(2,1)} %refs_3_.1, bf16[2,512]{1,0:T(2,128)(2,1)} %refs_4_.1, bf16[2,512]{1,0:T(2,128)(2,1)} %refs_5_.1, bf16[2,512,512]{2,1,0:T(8,128)(2,1)} %refs_6_.1, ...), custom_call_target="tpu_custom_call" | custom-call | tf_op jit(solution)/shard_map/pallas_call | solution.py:568
  70.2 1.6 %copy.20 = bf16[128,512]{1,0:T(8,128)(2,1)} copy(bf16[128,512]{1,0:T(8,128)(2,1)} %shard_map.163) | data formatting | bytes 262144

commit v12 on v11

--- a/solution.py
+++ b/solution.py
@@ -286,10 +286,12 @@
             project_partner_memory()
         phase(f'xwait{layer}')
 
-        @pl.when(chip == 0)
-        def _():
+        def forward_first():
             x_arrival(layer, CORES + core, 1).wait_recv()
             x_forward_first(layer).start()
+
+        if layer == 0:
+            pl.when(chip == 0)(forward_first)
 
         for turn in range(chips - 1):
             @pl.when(turn < chip)
@@ -369,6 +371,8 @@
             def _():
                 q_copy(layer, d, k).start()
         q_all[layer, me] = q_send[layer, core]
+        if layer > 0:
+            pl.when(chip == 0)(forward_first)
         later = []
         if layer == 0:
             later = [(0, name) for name in ('mlp_gate', 'mlp_up', 'mlp_down')]

time: 71.9 us -> 73.2 us (1.018)
  Pallas kernels: 69.6 us -> 70.8 us
    pallas_call x1, Pallas kernels: 69.6 us -> 70.8 us  [local_step(): pl.pallas_call(functools.partial(kernel, group, n_layers, head_dim), out_...]
where the time goes in v12:
time: 73.2 us; the launch traced here: 73.1 us
  Pallas kernels  70.8 us (97%)
  local copies, waits for them, and re-layouts  1.57 us (2%)
    pallas_call x1, Pallas kernels, local_step(): pl.pallas_call(functools.partial(kernel, group, n_layers, head_dim), out_...  70.8 us
    unnamed x1, local copies, waits for them, and re-layouts  1.57 us

profile of v12, /device:TPU:127, one launch (start us, length us, event | category | flops | bytes accessed | tf_op | source)
XLA Modules:
  0.0 73.1 jit_solution(9135610573435421618)
XLA Ops:
  0.7 70.8 %shard_map.163 = bf16[128,512]{1,0:T(8,128)(2,1)} custom-call(bf16[128,512]{1,0:T(8,128)(2,1)} %refs_0_.1, bf16[1024,512]{1,0:T(8,128)(2,1)} %refs_1_.1, s32[1]{0:T(128)S(6)} %copy.19.refs_2_, bf16[2,512]{1,0:T(2,128)(2,1)} %refs_3_.1, bf16[2,512]{1,0:T(2,128)(2,1)} %refs_4_.1, bf16[2,512]{1,0:T(2,128)(2,1)} %refs_5_.1, bf16[2,512,512]{2,1,0:T(8,128)(2,1)} %refs_6_.1, ...), custom_call_target="tpu_custom_call" | custom-call | tf_op jit(solution)/shard_map/pallas_call | solution.py:572
  71.5 1.6 %copy.20 = bf16[128,512]{1,0:T(8,128)(2,1)} copy(bf16[128,512]{1,0:T(8,128)(2,1)} %shard_map.163) | data formatting | bytes 262144
